TPU v7x, 32 devices: a whole 2x2x4 slice. The times are simulated.
32 devices in a mesh: gx: 8 (over y, x, core), gy: 4 (over z).
Axes of the slice: x: 2, y: 2, z: 4, core: 2. Of those that a mesh axis runs over, the one named last changes fastest.
Arguments:
- rhs_conc: float32 [16, 64, 2048], P('gx', 'gy'), may hold values from -60 to 60
- rhs_pots: float32 [16, 64, 33], P('gx', 'gy'), may hold values from -60 to 60
- diffusion: float32 [16, 64, 32], P('gx', 'gy'), may hold values from 0.05 to 5
- exchange: float32 [16, 64, 32], P('gx', 'gy'), may hold values from 0.2 to 4
- slope: float32 [16, 64, 32], P('gx', 'gy'), may hold values from 0.1 to 1
Outputs:
- sol_conc: float32 [16, 64, 2048], P('gx', 'gy')
- sol_pots: float32 [16, 64, 33], P('gx', 'gy')
All inputs are finite; a program needn't handle non-finite values.
Results may differ from a plain program's by a relative error of at most 0.0003.
Values sent between devices are 32-bit elements; how exact they have to be, the bound alone decides.
No kernel may reach another device: no remote copies, remote signals or barrier semaphores. Data moves between devices by JAX's collectives and lax.ppermute only.
A program may use at most 64 MiB of HBM per device.

v0:
```python
import jax
import jax.numpy as jnp
from jax import lax
from jax.sharding import PartitionSpec as P

ITERS = 10


node_cond = 1.0
plane_cond = 0.5
collector_cond = 2.0
epsilon = 1e-06


def padded_2(cells, sides, width):
    for axis, dim in sides:
        count = lax.axis_size(axis)
        ends = count - 1
        head = lax.slice_in_dim(cells, 0, width, axis=dim)
        tail = lax.slice_in_dim(cells, cells.shape[dim] - width, cells.shape[dim], axis=dim)
        cells = jnp.concatenate(
            [
                lax.ppermute(tail, axis, [(i, (i + 1) % count) for i in range(ends)]),
                cells,
                lax.ppermute(head, axis, [((i + 1) % count, i) for i in range(ends)]),
            ],
            axis=dim,
        )
    return cells


def mirror_laplace(values):
    inner = jnp.concatenate([values[..., :1], values[..., :-1]], axis=-1)
    outer = jnp.concatenate([values[..., 1:], values[..., -1:]], axis=-1)
    return 2.0 * values - inner - outer


def local_operator(conc, padded, diffusion, exchange, slope):
    nodes = exchange.shape[2]
    shell_count = conc.shape[2] // nodes
    shells = conc.reshape(conc.shape[0], conc.shape[1], nodes, shell_count)
    center = padded[1:-1, 1:-1]
    lateral = (
        4.0 * center - padded[2:, 1:-1] - padded[:-2, 1:-1] - padded[1:-1, 2:] - padded[1:-1, :-2]
    )
    node_pot = center[..., :nodes]
    collector = center[..., nodes]
    current = exchange * (node_pot - collector[..., None])
    surface = shells[..., shell_count - 1]
    surface_flag = (lax.broadcasted_iota(jnp.int32, (shell_count,), 0) == shell_count - 1).astype(
        jnp.float32
    )
    new_shells = (
        shells + diffusion[..., None] * mirror_laplace(shells) + current[..., None] * surface_flag
    )
    new_nodes = (
        node_cond * mirror_laplace(node_pot)
        + current
        - slope * surface
        + plane_cond * lateral[..., :nodes]
    )
    new_collector = collector_cond * lateral[..., nodes] - jnp.mean(current, axis=-1)
    return (
        new_shells.reshape(conc.shape),
        jnp.concatenate([new_nodes, new_collector[..., None]], axis=-1),
    )


def least_squares(columns, start_norm):
    count = len(columns)
    target = [start_norm] + [jnp.zeros_like(start_norm) for step in range(count)]
    cosines = []
    sines = []
    upper_rows = []
    for step in range(count):
        entries = list(columns[step])
        for row in range(step):
            first = cosines[row] * entries[row] + sines[row] * entries[row + 1]
            second = cosines[row] * entries[row + 1] - sines[row] * entries[row]
            entries[row] = first
            entries[row + 1] = second
        radius = jnp.sqrt(entries[step] * entries[step] + entries[step + 1] * entries[step + 1])
        cosine = entries[step] / radius
        sine = entries[step + 1] / radius
        entries[step] = radius
        cosines.append(cosine)
        sines.append(sine)
        lead = target[step]
        target[step] = cosine * lead
        target[step + 1] = -sine * lead
        upper_rows.append(entries[: step + 1])
    weights = [None] * count
    for row in range(count - 1, -1, -1):
        total = target[row]
        for later in range(row + 1, count):
            total = total - upper_rows[later][row] * weights[later]
        weights[row] = total / upper_rows[row][row]
    return weights


def shards(rhs_conc, rhs_pots, diffusion, exchange, slope):
    local_square = jnp.sum(rhs_conc * rhs_conc) + jnp.sum(rhs_pots * rhs_pots)
    start_norm = jnp.sqrt(lax.psum(local_square, ("gx", "gy")) + epsilon)
    basis = [(rhs_conc / start_norm, rhs_pots / start_norm)]
    columns = []
    for step in range(ITERS):
        padded = padded_2(basis[step][1], (("gx", 0), ("gy", 1)), 1)
        image_conc, image_pots = local_operator(basis[step][0], padded, diffusion, exchange, slope)
        local_dots = jnp.stack(
            [jnp.sum(vector[0] * image_conc) + jnp.sum(vector[1] * image_pots) for vector in basis]
        )
        image_square = jnp.sum(image_conc * image_conc) + jnp.sum(image_pots * image_pots)
        coeffs, total_square = lax.psum((local_dots, image_square), ("gx", "gy"))
        rest_conc, rest_pots = (image_conc, image_pots)
        for row in range(step + 1):
            rest_conc = rest_conc - coeffs[row] * basis[row][0]
            rest_pots = rest_pots - coeffs[row] * basis[row][1]
        height = jnp.sqrt(total_square - jnp.sum(coeffs * coeffs) + epsilon)
        basis.append((rest_conc / height, rest_pots / height))
        columns.append([coeffs[row] for row in range(step + 1)] + [height])
    weights = least_squares(columns, start_norm)
    sol_conc = weights[0] * basis[0][0]
    sol_pots = weights[0] * basis[0][1]
    for step in range(1, ITERS):
        sol_conc = sol_conc + weights[step] * basis[step][0]
        sol_pots = sol_pots + weights[step] * basis[step][1]
    return (sol_conc, sol_pots)


def solution(mesh):
    return jax.shard_map(
        shards,
        mesh=mesh,
        in_specs=(
            P("gx", "gy", None),
            P("gx", "gy", None),
            P("gx", "gy", None),
            P("gx", "gy", None),
            P("gx", "gy", None),
        ),
        out_specs=(P("gx", "gy", None), P("gx", "gy", None)),
        check_vma=False,
    )
```

profile of v0, /device:TPU:0, one launch (start us, length us, event | category | flops | bytes accessed | tf_op | source)
XLA Modules:
  0.0 950.6 jit_solution(5201951569017878183)
XLA Ops:
  2.0 1.7 multiply_reduce_fusion.65
  5.1 42.0 %psum.147 = f32[]{:T(128)} all-reduce(f32[]{:T(128)S(6)} %add.632), channel_id=1, replica_groups=mesh['gx'=8,'gy'=4] {'gx','gy'}, use_global_device_ids=true, to_apply=%region_2.0 | all-reduce | flops 1 | bytes 8 | tf_op jit(solution)/shard_map/psum | solution.py:103
  49.2 3.0 collective-permute-start.1
  57.7 4.5 collective-permute-start.3
  62.7 1.5 collective-permute-done.3
  69.2 42.0 %all-reduce.9 = (f32[]{:T(128)}, f32[1]{0:T(128)}) all-reduce(f32[]{:T(128)S(6)} %add.639, f32[1]{0:T(128)} %bitcast.3), channel_id=1, replica_groups=mesh['gx'=8,'gy'=4] {'gx','gy'}, use_global_device_ids=true, to_apply=%region_9.0 | all-reduce | flops 2 | bytes 16 | tf_op jit(solution)/shard_map/psum | solution.py:113
  116.6 3.0 collective-permute-start.5
  124.6 4.5 collective-permute-start.7
  129.5 1.5 collective-permute-done.7
  137.5 42.3 %all-reduce.8 = (f32[]{:T(128)}, f32[2]{0:T(128)S(1)}) all-reduce(f32[]{:T(128)S(6)} %add.649, f32[2]{0:T(128)S(1)} %pad_maximum_fusion.120), channel_id=1, replica_groups=mesh['gx'=8,'gy'=4] {'gx','gy'}, use_global_device_ids=true, to_apply=%region_18.0 | all-reduce | flops 3 | bytes 24 | tf_op jit(solution)/shard_map/psum | solution.py:113
  187.5 3.0 collective-permute-start.9
  196.1 4.7 collective-permute-start.11
  210.8 41.6 %all-reduce.7 = (f32[]{:T(128)}, f32[3]{0:T(128)S(1)}) all-reduce(f32[]{:T(128)S(6)} %add.660, f32[3]{0:T(128)S(1)} %pad_maximum_fusion.121), channel_id=1, replica_groups=mesh['gx'=8,'gy'=4] {'gx','gy'}, use_global_device_ids=true, to_apply=%region_30.0 | all-reduce | flops 4 | bytes 32 | tf_op jit(solution)/shard_map/psum | solution.py:113
  255.0 1.9 subtract_divide_fusion.15
  258.1 1.9 subtract_divide_fusion.6
  262.0 3.0 collective-permute-start.13
  271.7 4.5 collective-permute-start.15
  287.7 41.9 %all-reduce.6 = (f32[]{:T(128)}, f32[4]{0:T(128)S(1)}) all-reduce(f32[]{:T(128)S(6)} %add.672, f32[4]{0:T(128)S(1)} %pad_maximum_fusion.122), channel_id=1, replica_groups=mesh['gx'=8,'gy'=4] {'gx','gy'}, use_global_device_ids=true, to_apply=%region_44.0 | all-reduce | flops 5 | bytes 40 | tf_op jit(solution)/shard_map/psum | solution.py:113
  332.2 2.6 subtract_divide_fusion.14
  336.7 2.7 subtract_divide_fusion.5
  341.3 3.0 collective-permute-start.17
  353.1 4.5 collective-permute-start.19
  358.1 1.5 collective-permute-done.19
  370.5 41.6 %all-reduce.5 = (f32[]{:T(128)}, f32[5]{0:T(128)S(1)}) all-reduce(f32[]{:T(128)S(6)} %add.685, f32[5]{0:T(128)S(1)} %stack.210), channel_id=1, replica_groups=mesh['gx'=8,'gy'=4] {'gx','gy'}, use_global_device_ids=true, to_apply=%region_60.0 | all-reduce | flops 6 | bytes 48 | tf_op jit(solution)/shard_map/psum | solution.py:113
  414.7 3.2 subtract_divide_fusion.13
  419.1 3.2 subtract_divide_fusion.4
  424.3 3.2 collective-permute-start.21
  438.2 4.5 collective-permute-start.23
  456.9 41.9 %all-reduce.4 = (f32[]{:T(128)}, f32[6]{0:T(128)S(1)}) all-reduce(f32[]{:T(128)S(6)} %add.699, f32[6]{0:T(128)S(1)} %stack.217), channel_id=1, replica_groups=mesh['gx'=8,'gy'=4] {'gx','gy'}, use_global_device_ids=true, to_apply=%region_78.0 | all-reduce | flops 7 | bytes 56 | tf_op jit(solution)/shard_map/psum | solution.py:113
  501.4 3.7 subtract_divide_fusion.12
  506.9 3.8 subtract_divide_fusion.3
  515.4 3.0 collective-permute-start.25
  530.8 4.5 collective-permute-start.27
  539.8 1.7 multiply_reduce_fusion.31
  551.5 41.6 %all-reduce.3 = (f32[]{:T(128)}, f32[7]{0:T(128)S(1)}) all-reduce(f32[]{:T(128)S(6)} %add.714, f32[7]{0:T(128)S(1)} %stack.225), channel_id=1, replica_groups=mesh['gx'=8,'gy'=4] {'gx','gy'}, use_global_device_ids=true, to_apply=%region_98.0 | all-reduce | flops 8 | bytes 64 | tf_op jit(solution)/shard_map/psum | solution.py:113
  595.8 4.4 subtract_divide_fusion.11
  602.2 4.5 subtract_divide_fusion.2
  611.8 2.1 copy.529
  615.2 3.6 collective-permute-start.29
  618.8 2.1 pad_maximum_fusion.15
  632.6 4.8 collective-permute-start.31
  645.6 2.6 multiply_reduce_fusion.22
  659.6 40.8 %all-reduce.2 = (f32[]{:T(128)}, f32[8]{0:T(128)S(1)}) all-reduce(f32[]{:T(128)S(6)} %add.730, f32[8]{0:T(128)S(1)} %stack.234), channel_id=1, replica_groups=mesh['gx'=8,'gy'=4] {'gx','gy'}, use_global_device_ids=true, to_apply=%region_120.0 | all-reduce | flops 9 | bytes 72 | tf_op jit(solution)/shard_map/psum | solution.py:113
  703.1 5.0 subtract_divide_fusion.10
  710.7 5.1 subtract_divide_fusion.1
  723.4 2.1 copy.530
  726.8 3.6 collective-permute-start.33
  730.4 2.1 pad_maximum_fusion.17
  738.6 1.9 concatenate.447
  743.7 4.5 collective-permute-start.35
  755.7 1.7 multiply_reduce_fusion.78
  757.3 2.1 multiply_reduce_fusion.12
  772.0 41.0 %all-reduce.1 = (f32[]{:T(128)}, f32[9]{0:T(128)S(1)}) all-reduce(f32[]{:T(128)S(6)} %add.747, f32[9]{0:T(128)S(1)} %stack.244), channel_id=1, replica_groups=mesh['gx'=8,'gy'=4] {'gx','gy'}, use_global_device_ids=true, to_apply=%region_144.0 | all-reduce | flops 10 | bytes 80 | tf_op jit(solution)/shard_map/psum | solution.py:113
  815.7 5.7 subtract_divide_fusion.9
  824.0 6.6 subtract_divide_fusion
  839.7 2.1 copy.531
  843.1 3.6 collective-permute-start.37
  846.8 2.0 pad_maximum_fusion.19
  856.9 1.9 concatenate.461
  861.6 4.5 collective-permute-start.39
  872.2 2.0 mul.2912
  874.2 1.7 multiply_reduce_fusion.66
  875.9 2.1 multiply_reduce_fusion
  891.7 40.8 %all-reduce = (f32[10]{0:T(128)S(1)}, f32[]{:T(128)}) all-reduce(f32[10]{0:T(128)S(1)} %stack.255, f32[]{:T(128)S(6)} %add.765), channel_id=1, replica_groups=mesh['gx'=8,'gy'=4] {'gx','gy'}, use_global_device_ids=true, to_apply=%region_167.0 | all-reduce | flops 11 | bytes 88 | tf_op jit(solution)/shard_map/psum | solution.py:113
  (492 shorter events, 152.6 us)
Async XLA Ops:
  0.6 4.4 copy-start.43
  2.0 50.2 %copy-start = (f32[2,16,2048]{2,1,0:T(8,128)S(1)}, f32[2,16,2048]{2,1,0:T(8,128)}, u32[]{:S(2)}) copy-start(f32[2,16,2048]{2,1,0:T(8,128)} %param.5) | copy-start | bytes 786436
  47.9 8.4 collective-permute-start
  49.2 7.1 collective-permute-start.1
  56.4 6.2 collective-permute-start.2
  57.7 6.5 collective-permute-start.3
  115.3 7.8 collective-permute-start.4
  116.6 6.5 collective-permute-start.5
  123.3 6.2 collective-permute-start.6
  124.6 6.5 collective-permute-start.7
  186.2 8.4 collective-permute-start.8
  187.5 7.1 collective-permute-start.9
  194.8 6.4 collective-permute-start.10
  196.1 6.5 collective-permute-start.11
  260.7 9.5 collective-permute-start.12
  262.0 8.2 collective-permute-start.13
  270.4 6.2 collective-permute-start.14
  271.7 6.5 collective-permute-start.15
  340.0 11.7 %collective-permute-start.16 = (f32[1,16,33]{1,0,2:T(1,128)}, f32[1,16,33]{1,0,2:T(1,128)S(1)}, u32[]{:S(2)}, u32[]{:S(2)}) collective-permute-start(f32[1,16,33]{1,0,2:T(1,128)} %get-tuple-element.304), channel_id=1, source_target_pairs={{4,0},{8,4},{12,8},{16,12},{20,16},{24,20},{28,24},{5,1},{9,5},{13... | collective-permute-start | bytes 6344 | tf_op jit(solution)/shard_map/ppermute | solution.py:25
  341.3 10.4 %collective-permute-start.17 = (f32[1,16,33]{1,0,2:T(1,128)}, f32[1,16,33]{1,0,2:T(1,128)S(1)}, u32[]{:S(2)}, u32[]{:S(2)}) collective-permute-start(f32[1,16,33]{1,0,2:T(1,128)} %get-tuple-element.303), channel_id=1, source_target_pairs={{0,4},{4,8},{8,12},{12,16},{16,20},{20,24},{24,28},{1,5},{5,9},{9,... | collective-permute-start | bytes 6344 | tf_op jit(solution)/shard_map/ppermute | solution.py:23
  351.8 6.2 collective-permute-start.18
  353.1 6.5 collective-permute-start.19
  423.0 13.7 %collective-permute-start.20 = (f32[1,16,33]{1,0,2:T(1,128)S(1)}, f32[1,16,33]{1,0,2:T(1,128)S(1)}, u32[]{:S(2)}, u32[]{:S(2)}) collective-permute-start(f32[1,16,33]{1,0,2:T(1,128)S(1)} %get-tuple-element.297), channel_id=1, source_target_pairs={{4,0},{8,4},{12,8},{16,12},{20,16},{24,20},{28,24},{5,1},{9,5},{13... | collective-permute-start | bytes 6344 | tf_op jit(solution)/shard_map/ppermute | solution.py:25
  424.3 12.4 %collective-permute-start.21 = (f32[1,16,33]{1,0,2:T(1,128)S(1)}, f32[1,16,33]{1,0,2:T(1,128)S(1)}, u32[]{:S(2)}, u32[]{:S(2)}) collective-permute-start(f32[1,16,33]{1,0,2:T(1,128)S(1)} %get-tuple-element.296), channel_id=1, source_target_pairs={{0,4},{4,8},{8,12},{12,16},{16,20},{20,24},{24,28},{1,5},{5,9},{9,... | collective-permute-start | bytes 6344 | tf_op jit(solution)/shard_map/ppermute | solution.py:23
  429.8 6.7 copy-start.9
  436.9 6.2 collective-permute-start.22
  438.2 6.5 collective-permute-start.23
  443.1 1.9 copy-start.40
  514.1 15.2 %collective-permute-start.24 = (f32[1,16,33]{1,0,2:T(1,128)}, f32[1,16,33]{1,0,2:T(1,128)S(1)}, u32[]{:S(2)}, u32[]{:S(2)}) collective-permute-start(f32[1,16,33]{1,0,2:T(1,128)} %get-tuple-element.289), channel_id=1, source_target_pairs={{4,0},{8,4},{12,8},{16,12},{20,16},{24,20},{28,24},{5,1},{9,5},{13... | collective-permute-start | bytes 6344 | tf_op jit(solution)/shard_map/ppermute | solution.py:25
  515.4 13.9 %collective-permute-start.25 = (f32[1,16,33]{1,0,2:T(1,128)}, f32[1,16,33]{1,0,2:T(1,128)S(1)}, u32[]{:S(2)}, u32[]{:S(2)}) collective-permute-start(f32[1,16,33]{1,0,2:T(1,128)} %get-tuple-element.288), channel_id=1, source_target_pairs={{0,4},{4,8},{8,12},{12,16},{16,20},{20,24},{24,28},{1,5},{5,9},{9,... | collective-permute-start | bytes 6344 | tf_op jit(solution)/shard_map/ppermute | solution.py:23
  529.5 6.2 collective-permute-start.26
  530.8 6.5 collective-permute-start.27
  535.7 1.9 copy-start.37
  535.7 1.9 copy-start.38
  595.8 6.4 copy-start.23
  609.2 9.5 %copy-start.3 = (f32[2,16,32,1]{3,2,1,0:T(8,128)S(1)}, f32[2,16,32,1]{3,2,1,0:T(8,128)}, u32[]{:S(2)}) copy-start(f32[2,16,32,1]{3,2,1,0:T(8,128)} %get-tuple-element.197) | copy-start | bytes 12292
  613.9 16.6 %collective-permute-start.28 = (f32[1,16,33]{1,0,2:T(1,128)}, f32[1,16,33]{1,0,2:T(1,128)S(1)}, u32[]{:S(2)}, u32[]{:S(2)}) collective-permute-start(f32[1,16,33]{1,0,2:T(1,128)} %get-tuple-element.280), channel_id=1, source_target_pairs={{4,0},{8,4},{12,8},{16,12},{20,16},{24,20},{28,24},{5,1},{9,5},{13... | collective-permute-start | bytes 6344 | tf_op jit(solution)/shard_map/ppermute | solution.py:25
  615.2 15.3 %collective-permute-start.29 = (f32[1,16,33]{1,0,2:T(1,128)}, f32[1,16,33]{1,0,2:T(1,128)}, u32[]{:S(2)}, u32[]{:S(2)}) collective-permute-start(f32[1,16,33]{1,0,2:T(1,128)} %get-tuple-element.279), channel_id=1, source_target_pairs={{0,4},{4,8},{8,12},{12,16},{16,20},{20,24},{24,28},{1,5},{5,9},{9,... | collective-permute-start | bytes 6344 | tf_op jit(solution)/shard_map/ppermute | solution.py:23
  618.8 2.1 copy-start.12
  618.8 2.1 copy-start.13
  621.9 7.6 copy-start.8
  631.3 7.2 collective-permute-start.30
  632.6 7.0 collective-permute-start.31
  638.5 2.2 copy-start.28
  638.5 2.2 copy-start.35
  638.5 2.2 copy-start.36
  703.1 7.6 copy-start.19
  718.4 12.0 %copy-start.2 = (f32[2,16,32,1]{3,2,1,0:T(8,128)S(1)}, f32[2,16,32,1]{3,2,1,0:T(8,128)}, u32[]{:S(2)}) copy-start(f32[2,16,32,1]{3,2,1,0:T(8,128)} %get-tuple-element.193) | copy-start | bytes 12292
  725.5 16.0 %collective-permute-start.32 = (f32[1,16,33]{1,0,2:T(1,128)}, f32[1,16,33]{1,0,2:T(1,128)}, u32[]{:S(2)}, u32[]{:S(2)}) collective-permute-start(f32[1,16,33]{1,0,2:T(1,128)} %get-tuple-element.270), channel_id=1, source_target_pairs={{4,0},{8,4},{12,8},{16,12},{20,16},{24,20},{28,24},{5,1},{9,5},{13... | collective-permute-start | bytes 6344 | tf_op jit(solution)/shard_map/ppermute | solution.py:25
  726.8 14.7 %collective-permute-start.33 = (f32[1,16,33]{1,0,2:T(1,128)}, f32[1,16,33]{1,0,2:T(1,128)}, u32[]{:S(2)}, u32[]{:S(2)}) collective-permute-start(f32[1,16,33]{1,0,2:T(1,128)} %get-tuple-element.269), channel_id=1, source_target_pairs={{0,4},{4,8},{8,12},{12,16},{16,20},{20,24},{24,28},{1,5},{5,9},{9,... | collective-permute-start | bytes 6344 | tf_op jit(solution)/shard_map/ppermute | solution.py:23
  730.4 2.1 copy-start.10
  730.4 2.1 copy-start.11
  733.6 7.0 copy-start.7
  742.4 7.7 collective-permute-start.34
  743.7 7.0 collective-permute-start.35
  771.9 43.8 %copy-start.24 = (f32[2,16,32]{1,0,2:T(2,128)S(1)}, f32[2,16,32]{1,0,2:T(2,128)}, u32[]{:S(2)}) copy-start(f32[2,16,32]{1,0,2:T(2,128)} %get-tuple-element.161) | copy-start | bytes 12292
  821.4 2.0 copy-start.5
  834.1 12.7 %copy-start.1 = (f32[2,16,32,1]{3,2,1,0:T(8,128)S(1)}, f32[2,16,32,1]{3,2,1,0:T(8,128)}, u32[]{:S(2)}) copy-start(f32[2,16,32,1]{3,2,1,0:T(8,128)} %get-tuple-element.189) | copy-start | bytes 12292
  841.9 17.0 %collective-permute-start.36 = (f32[1,16,33]{1,0,2:T(1,128)}, f32[1,16,33]{1,0,2:T(1,128)}, u32[]{:S(2)}, u32[]{:S(2)}) collective-permute-start(f32[1,16,33]{1,0,2:T(1,128)} %get-tuple-element.259), channel_id=1, source_target_pairs={{4,0},{8,4},{12,8},{16,12},{20,16},{24,20},{28,24},{5,1},{9,5},{13... | collective-permute-start | bytes 6344 | tf_op jit(solution)/shard_map/ppermute | solution.py:25
  843.1 15.7 %collective-permute-start.37 = (f32[1,16,33]{1,0,2:T(1,128)}, f32[1,16,33]{1,0,2:T(1,128)}, u32[]{:S(2)}, u32[]{:S(2)}) collective-permute-start(f32[1,16,33]{1,0,2:T(1,128)} %get-tuple-element.258), channel_id=1, source_target_pairs={{0,4},{4,8},{8,12},{12,16},{16,20},{20,24},{24,28},{1,5},{5,9},{9,... | collective-permute-start | bytes 6344 | tf_op jit(solution)/shard_map/ppermute | solution.py:23
  856.9 1.9 copy-start.6
  860.3 7.7 collective-permute-start.38
  861.6 7.0 collective-permute-start.39
  872.2 3.7 copy-start.20
  (39 other events, 45.7 us)
where the time goes:
time: 965 us; the launch traced here: 951 us
  blocking collectives  457 us (47%)
  between operations  171 us (18%)
  other arithmetic  118 us (12%)
  starting transfers between devices  104 us (11%)
  local copies, waits for them, and re-layouts  87.2 us (9%)
  waiting for transfers between devices  12.9 us (1%)
    psum x10, blocking collectives, shards(): coeffs, total_square = lax.psum((local_dots, image_square), ('gx', 'gy'))  415 us
    ppermute x20, starting transfers between devices, padded_2(): lax.ppermute(tail, axis, [(i, (i + 1) % count) for i in range(ends)])  78.2 us
    div x18, other arithmetic, shards(): basis.append((rest_conc / height, rest_pots / height))  58.3 us
    psum x1, blocking collectives, shards(): start_norm = jnp.sqrt(lax.psum(local_square, ('gx', 'gy')) + epsilon)  42 us
    ppermute x20, starting transfers between devices, padded_2(): lax.ppermute(head, axis, [((i + 1) % count, i) for i in range(ends)])  25.8 us
  transfers between devices with their start and end apart: 40, of which 10 were waited for; matrix products, arithmetic and copies ran while one was open for 4% of the time, Pallas kernels for 0%

commit v1 on v0

v1 whole, which is shorter than its diff:
```python
import functools

import jax
import jax.numpy as jnp
from jax import lax
from jax.experimental import pallas as pl
from jax.experimental.pallas import tpu as pltpu
from jax.sharding import PartitionSpec as P

ITERS = 10
NR = 64
LANES = 128

node_cond = 1.0
plane_cond = 0.5
collector_cond = 2.0
epsilon = 1e-06

CENTER = 10.45
HALF = 9.55
INVERSE_MAX = 5.0e3
NORM_MIN = 1.0

KV = ITERS + 1
PAIRS = KV * (KV + 1) // 2
SHELLS = ITERS - 1
FIELDS = 5 + SHELLS


def lanes_of(shape):
    return lax.broadcasted_iota(jnp.int32, shape, len(shape) - 1)


def pick(values, index):
    return jnp.take_along_axis(values, index, axis=1, mode="promise_in_bounds")


def pack_kernel(conc_ref, pots_ref, diff_ref, exch_ref, slope_ref, send_ref, deep_ref):
    rows, ys, nodes = exch_ref.shape
    half = rows * nodes
    lane = lanes_of((ys, LANES))

    def join(ref):
        return jnp.concatenate([ref[x][:, :nodes] for x in range(rows)], axis=1)

    collector = jnp.concatenate(
        [jnp.broadcast_to(pots_ref[x][:, nodes : nodes + 1], (ys, nodes)) for x in range(rows)],
        axis=1,
    )
    plain = [join(pots_ref), collector, join(diff_ref), join(exch_ref), join(slope_ref)]
    node = lane % half
    shells = [jnp.zeros((ys, LANES), jnp.float32) for k in range(SHELLS + 1)]
    for x in range(rows):
        for tile in range(nodes * NR // LANES):
            cells = conc_ref[x, :, tile * LANES : (tile + 1) * LANES]
            here = (node // 2) == (x * nodes // 2 + tile)
            for k in range(SHELLS + 1):
                found = pick(cells, (node % 2) * NR + (NR - 1 - k))
                shells[k] = jnp.where(here, found, shells[k])
    low = lane < half
    send_ref[0] = jnp.concatenate([plain[0], plain[1]], axis=1)
    send_ref[1] = jnp.concatenate([plain[2], plain[3]], axis=1)
    send_ref[2] = jnp.where(low, jnp.concatenate([plain[4], plain[4]], axis=1), shells[0])
    for k in range(1, SHELLS, 2):
        send_ref[2 + (k + 1) // 2] = jnp.where(low, shells[k], shells[k + 1])
    deep_ref[...] = shells[SHELLS]


def powers_kernel(
    spot_ref, conc_ref, diff_ref, own_ref, left_ref, right_ref, deep_ref,
    basis_ref, gram_ref,
    field_ref, current_ref, dexp_ref, acc_ref,
):
    rows, ys, nodes = diff_ref.shape
    blocks = own_ref.shape[0]
    half = rows * nodes
    reach = left_ref.shape[2]
    quads = blocks // 2
    window = field_ref.shape[2]
    spot = spot_ref[0]
    quad = spot // 2
    odd = (spot % 2) == 1
    lane2 = lanes_of((ys, LANES))

    field_ref[...] = jnp.zeros(field_ref.shape, jnp.float32)
    for source, start, count in ((own_ref, 0, ys), (right_ref, ys, reach), (left_ref, window - reach, reach)):
        low = lanes_of((count, LANES)) < half
        for field in range(FIELDS):
            for q in range(quads):
                a = source[2 * q, field // 2]
                b = source[2 * q + 1, field // 2]
                if field % 2 == 0:
                    value = jnp.where(low, a, pltpu.roll(b, half, 1))
                else:
                    value = jnp.where(low, pltpu.roll(a, half, 1), b)
                field_ref[field, q, start : start + count, :] = value
    field_ref[FIELDS, quad, 0:ys, :] = deep_ref[...]

    shape = (quads, window, LANES)
    flat = (quads * window, LANES)
    lane = lanes_of(shape)
    diff = field_ref[2]
    exch = field_ref[3]
    slope = field_ref[4]
    inside = exch > 0.0
    first = (lane % nodes) == 0
    last = (lane % nodes) == (nodes - 1)
    block = (lax.broadcasted_iota(jnp.int32, (LANES, LANES), 0) // nodes) == (
        lanes_of((LANES, LANES)) // nodes
    )
    mean_mat = jnp.where(block, 1.0 / nodes, 0.0)

    def lroll(value, shift):
        return pltpu.roll(value.reshape(flat), shift % LANES, 1).reshape(shape)

    def plane(value):
        up = lroll(value, -nodes)
        down = lroll(value, nodes)
        zero = jnp.zeros((1, window, LANES), jnp.float32)
        up_next = jnp.concatenate([up[1:], zero], axis=0)
        down_prev = jnp.concatenate([zero, down[:-1]], axis=0)
        xp = jnp.where(lane < LANES - nodes, up, up_next)
        xm = jnp.where(lane >= nodes, down, down_prev)
        yp = jnp.stack([pltpu.roll(value[q], window - 1, 0) for q in range(quads)])
        ym = jnp.stack([pltpu.roll(value[q], 1, 0) for q in range(quads)])
        return 4.0 * value - xp - xm - yp - ym

    def own_of(ref_value):
        return jnp.where(odd, pltpu.roll(ref_value, half, 1), ref_value)

    pots = field_ref[0]
    coll = field_ref[1]
    shells = [field_ref[5 + k] for k in range(SHELLS + 1)]
    old_pots, old_coll, old_shells = None, None, None
    low2 = lane2 < half
    head = (lane2 % nodes) == 0

    for step in range(KV):
        field_ref[0] = pots
        field_ref[1] = coll
        own_p = own_of(field_ref[0, quad, 0:ys, :])
        own_v = own_of(field_ref[1, quad, 0:ys, :])
        tile = jnp.where(low2, own_p, jnp.where(head, pltpu.roll(own_v, half, 1), 0.0))
        basis_ref[step, basis_ref.shape[1] - 1] = tile
        if step == ITERS:
            break
        flow = exch * (pots - coll)
        field_ref[2] = flow
        current_ref[step] = own_of(field_ref[2, quad, 0:ys, :])
        mean = jnp.dot(
            flow.reshape(flat), mean_mat, precision=lax.Precision.HIGHEST,
            preferred_element_type=jnp.float32,
        ).reshape(shape)
        inner = jnp.where(first, pots, lroll(pots, 1))
        outer = jnp.where(last, pots, lroll(pots, -1))
        image_p = (
            node_cond * (2.0 * pots - inner - outer)
            + flow
            - slope * shells[0]
            + plane_cond * plane(pots)
        )
        image_v = collector_cond * plane(coll) - mean
        keep = SHELLS - step
        image_s = []
        for k in range(keep):
            if k == 0:
                image_s.append(shells[0] + diff * (shells[0] - shells[1]) + flow)
            else:
                image_s.append(
                    shells[k] + diff * (2.0 * shells[k] - shells[k + 1] - shells[k - 1])
                )
        scale = (1.0 if step == 0 else 2.0) / HALF

        def recur(image, now, old):
            value = scale * (image - CENTER * now)
            return value if old is None else value - old

        new_pots = jnp.where(inside, recur(image_p, pots, old_pots), 0.0)
        new_coll = jnp.where(inside, recur(image_v, coll, old_coll), 0.0)
        new_shells = [
            recur(image_s[k], shells[k], None if old_shells is None else old_shells[k])
            for k in range(keep)
        ]
        old_pots, old_coll, old_shells = pots, coll, shells
        pots, coll, shells = new_pots, new_coll, new_shells

    tiles = nodes * NR // LANES
    upper = lane2 // NR
    surface = (lane2 % NR) == (NR - 1)
    bottom = (lane2 % NR) == 0
    for x in range(rows):
        packed = jnp.concatenate([diff_ref[x]] * (LANES // nodes), axis=1)
        for tile in range(tiles):
            dexp_ref[x * tiles + tile] = pick(packed, 2 * tile + upper)
            basis_ref[0, x * tiles + tile] = conc_ref[x, :, tile * LANES : (tile + 1) * LANES]

    def advance(step, carry):
        gain = jnp.where(step == 0, 1.0 / HALF, 2.0 / HALF)
        back = jnp.where(step == 0, 0.0, 1.0)
        before = jnp.maximum(step - 1, 0)
        flow = current_ref[step]
        for x in range(rows):
            for tile in range(tiles):
                at = x * tiles + tile
                now = basis_ref[step, at]
                old = basis_ref[before, at]
                inner = jnp.where(bottom, now, pltpu.roll(now, 1, 1))
                outer = jnp.where(surface, now, pltpu.roll(now, LANES - 1, 1))
                source = jnp.where(surface, pick(flow, x * nodes + 2 * tile + upper), 0.0)
                image = now + dexp_ref[at] * (2.0 * now - inner - outer) + source
                basis_ref[step + 1, at] = gain * (image - CENTER * now) - back * old
        return carry

    lax.fori_loop(0, ITERS, advance, 0)

    acc_ref[...] = jnp.zeros(acc_ref.shape, jnp.float32)
    count = basis_ref.shape[1]

    def gather_gram(at, carry):
        cells = [basis_ref[k, at] for k in range(KV)]
        pair = 0
        for i in range(KV):
            for j in range(i, KV):
                product = cells[i] * cells[j]
                acc_ref[pair] += product[:8] + product[8:]
                pair += 1
        return carry

    lax.fori_loop(0, count, gather_gram, 0)
    sums = jnp.sum(acc_ref[...], axis=1)
    gram_ref[...] = lax.dot_general(
        jnp.ones((gram_ref.shape[0], LANES), jnp.float32), sums, (((1,), (1,)), ((), ())),
        precision=lax.Precision.HIGHEST, preferred_element_type=jnp.float32,
    )


def solve_kernel(sums_ref, basis_ref, conc_ref, pots_ref, flag_ref):
    rows, ys, width = conc_ref.shape
    nodes = pots_ref.shape[2] - 1
    half = rows * nodes
    tiles = width // LANES
    side = 16
    total = jnp.sum(sums_ref[...], axis=0, keepdims=True)
    shape = (side, LANES)
    row = lax.broadcasted_iota(jnp.int32, shape, 0)
    col = lanes_of(shape)
    small = jnp.minimum(row, col)
    large = jnp.maximum(row, col)
    index = small * KV - (small * (small - 1)) // 2 + (large - small)
    valid = (row < KV) & (col < KV)
    index = jnp.where(valid, index, 0)
    gram = jnp.where(valid, pick(jnp.broadcast_to(total, shape), index), 0.0)
    eye = (row == col).astype(jnp.float32)

    def lane_sum(value):
        return jnp.sum(value, axis=1, keepdims=True)

    def sub_sum(value):
        return jnp.sum(value, axis=0, keepdims=True)

    column = (side, 1)
    crow = lax.broadcasted_iota(jnp.int32, column, 0)
    norm0 = gram[0:1, 0:1]
    beta = jnp.sqrt(norm0 + epsilon)
    coeffs = []
    images = []
    q = jnp.where(crow == 0, 1.0, 0.0) / beta
    gq = lane_sum(jnp.where(col == 0, gram, 0.0)) / beta
    table = jnp.where(col == 0, q, 0.0)
    gtable = jnp.where(col == 0, gq, 0.0)
    diag = lane_sum(gram * eye)
    columns = []
    coeffs.append(q)
    worst = jnp.zeros((1, 1), jnp.float32)
    for step in range(ITERS):
        down = pltpu.roll(jnp.broadcast_to(q, shape), 1, 0)
        up = jnp.where(
            row < side - 1, pltpu.roll(jnp.broadcast_to(q, shape), side - 1, 0), 0.0
        )
        q_full = jnp.broadcast_to(q, shape)
        first = jnp.broadcast_to(q[0:1], shape)
        w = CENTER * q_full + (0.5 * HALF) * (down + up) + jnp.where(
            row == 1, (0.5 * HALF) * first, 0.0
        )
        w_row = sub_sum(eye * w)
        g = lane_sum(gram * w_row)
        h_row = sub_sum(table * g)
        u = w[:, 0:1] - lane_sum(table * h_row)
        gu = g - lane_sum(gtable * h_row)
        square = sub_sum(u * gu)
        height = jnp.sqrt(square + epsilon)
        inverse = 1.0 / height
        q = u * inverse
        gq = gu * inverse
        columns.append(
            [lane_sum(jnp.where(lanes_of((1, LANES)) == i, h_row, 0.0)) for i in range(step + 1)]
            + [height]
        )
        coeffs.append(q)
        if step < ITERS - 1:
            table = jnp.where(col == step + 1, q, table)
            gtable = jnp.where(col == step + 1, gq, gtable)
        worst = jnp.maximum(worst, sub_sum(q * q * diag))
    good = (worst < INVERSE_MAX) & (norm0 > NORM_MIN)
    weights = least_squares(columns, beta)
    mix = weights[0] * coeffs[0]
    for step in range(1, ITERS):
        mix = mix + weights[step] * coeffs[step]
    bad = jnp.where(good & (jnp.abs(sub_sum(mix)) < 1e30), 0, 1)
    flag_ref[0] = jnp.max(bad)
    mix_full = jnp.broadcast_to(mix, shape)
    parts = [jnp.broadcast_to(mix_full[k : k + 1], (ys, LANES)) for k in range(ITERS)]

    def combine(at):
        value = parts[0] * basis_ref[0, at]
        for k in range(1, ITERS):
            value = value + parts[k] * basis_ref[k, at]
        return value

    for x in range(rows):
        for tile in range(tiles):
            conc_ref[x, :, tile * LANES : (tile + 1) * LANES] = combine(x * tiles + tile)
    last = combine(rows * tiles)
    for x in range(rows):
        pots_ref[x] = jnp.concatenate(
            [
                last[:, x * nodes : (x + 1) * nodes],
                last[:, half + x * nodes : half + x * nodes + 1],
            ],
            axis=1,
        )


def least_squares(columns, start_norm):
    count = len(columns)
    target = [start_norm] + [jnp.zeros_like(start_norm) for step in range(count)]
    cosines = []
    sines = []
    upper_rows = []
    for step in range(count):
        entries = list(columns[step])
        for row in range(step):
            first = cosines[row] * entries[row] + sines[row] * entries[row + 1]
            second = cosines[row] * entries[row + 1] - sines[row] * entries[row]
            entries[row] = first
            entries[row + 1] = second
        radius = jnp.sqrt(entries[step] * entries[step] + entries[step + 1] * entries[step + 1])
        cosine = entries[step] / radius
        sine = entries[step + 1] / radius
        entries[step] = radius
        cosines.append(cosine)
        sines.append(sine)
        lead = target[step]
        target[step] = cosine * lead
        target[step + 1] = -sine * lead
        upper_rows.append(entries[: step + 1])
    weights = [None] * count
    for row in range(count - 1, -1, -1):
        total = target[row]
        for later in range(row + 1, count):
            total = total - upper_rows[later][row] * weights[later]
        weights[row] = total / upper_rows[row][row]
    return weights


def shifted(cells, axis, dim):
    count = lax.axis_size(axis)
    size = cells.shape[dim]
    head = lax.slice_in_dim(cells, 0, 1, axis=dim)
    tail = lax.slice_in_dim(cells, size - 1, size, axis=dim)
    before = lax.ppermute(tail, axis, [(i, i + 1) for i in range(count - 1)])
    after = lax.ppermute(head, axis, [(i + 1, i) for i in range(count - 1)])
    padded = jnp.concatenate([before, cells, after], axis=dim)
    return lax.slice_in_dim(padded, 0, size, axis=dim), lax.slice_in_dim(padded, 2, size + 2, axis=dim)


def mirror_laplace(values):
    inner = jnp.concatenate([values[..., :1], values[..., :-1]], axis=-1)
    outer = jnp.concatenate([values[..., 1:], values[..., -1:]], axis=-1)
    return 2.0 * values - inner - outer


def local_operator(conc, pots, diffusion, exchange, slope):
    nodes = exchange.shape[2]
    shells = conc.reshape(conc.shape[0], conc.shape[1], nodes, NR)
    xm, xp = shifted(pots, "gx", 0)
    ym, yp = shifted(pots, "gy", 1)
    lateral = 4.0 * pots - xm - xp - ym - yp
    node_pot = pots[..., :nodes]
    current = exchange * (node_pot - pots[..., nodes:])
    flag = (lax.broadcasted_iota(jnp.int32, (NR,), 0) == NR - 1).astype(jnp.float32)
    new_shells = shells + diffusion[..., None] * mirror_laplace(shells) + current[..., None] * flag
    new_nodes = (
        node_cond * mirror_laplace(node_pot)
        + current
        - slope * shells[..., NR - 1]
        + plane_cond * lateral[..., :nodes]
    )
    new_collector = collector_cond * lateral[..., nodes:] - jnp.mean(current, axis=-1, keepdims=True)
    return new_shells.reshape(conc.shape), jnp.concatenate([new_nodes, new_collector], axis=-1)


def weights_kernel(hess_ref, out_ref):
    def entry(i, j):
        return hess_ref[j, i : i + 1, 0:1]

    columns = [[entry(i, j) for i in range(j + 2)] for j in range(ITERS)]
    start = hess_ref[ITERS, 0:1, 0:1]
    for k, weight in enumerate(least_squares(columns, start)):
        out_ref[k : k + 1, :] = jnp.broadcast_to(weight, (1, LANES))


def plain_cycle(rhs_conc, rhs_pots, diffusion, exchange, slope):
    axes = ("gx", "gy")
    square = jnp.sum(rhs_conc * rhs_conc) + jnp.sum(rhs_pots * rhs_pots)
    start = jnp.sqrt(lax.psum(square, axes) + epsilon)
    basis_c = jnp.zeros((KV,) + rhs_conc.shape, jnp.float32).at[0].set(rhs_conc / start)
    basis_p = jnp.zeros((KV,) + rhs_pots.shape, jnp.float32).at[0].set(rhs_pots / start)
    hess = jnp.zeros((KV, 16), jnp.float32).at[ITERS, 0].set(start)
    spot = jnp.arange(16)

    def body(step, carry):
        basis_c, basis_p, hess = carry
        conc = lax.dynamic_index_in_dim(basis_c, step, 0, False)
        pots = lax.dynamic_index_in_dim(basis_p, step, 0, False)
        image_c, image_p = local_operator(conc, pots, diffusion, exchange, slope)
        dots = jnp.sum(basis_c * image_c, axis=(1, 2, 3)) + jnp.sum(basis_p * image_p, axis=(1, 2, 3))
        dots = lax.psum(dots, axes)
        rest_c = image_c - jnp.sum(dots[:, None, None, None] * basis_c, axis=0)
        rest_p = image_p - jnp.sum(dots[:, None, None, None] * basis_p, axis=0)
        square = lax.psum(jnp.sum(rest_c * rest_c) + jnp.sum(rest_p * rest_p), axes)
        height = jnp.sqrt(square + epsilon)
        basis_c = lax.dynamic_update_index_in_dim(basis_c, rest_c / height, step + 1, 0)
        basis_p = lax.dynamic_update_index_in_dim(basis_p, rest_p / height, step + 1, 0)
        line = jnp.concatenate([dots, jnp.zeros((16 - KV,), jnp.float32)])
        line = jnp.where(spot == step + 1, height, line)
        hess = lax.dynamic_update_index_in_dim(hess, line, step, 0)
        return basis_c, basis_p, hess

    basis_c, basis_p, hess = lax.fori_loop(0, ITERS, body, (basis_c, basis_p, hess))
    wide = jnp.broadcast_to(hess[:, :, None], hess.shape + (LANES,))
    weights = pl.pallas_call(
        weights_kernel, out_shape=jax.ShapeDtypeStruct((16, LANES), jnp.float32)
    )(wide)[:KV, 0]
    weights = jnp.where(jnp.arange(KV) < ITERS, weights, 0.0)[:, None, None, None]
    return jnp.sum(weights * basis_c, axis=0), jnp.sum(weights * basis_p, axis=0)


def shards(rhs_conc, rhs_pots, diffusion, exchange, slope):
    rows, ys, nodes = exchange.shape
    gx, gy = lax.axis_size("gx"), lax.axis_size("gy")
    half = rows * nodes
    pairs = FIELDS // 2
    reach = ITERS
    assert half * 2 == LANES and nodes * NR == rhs_conc.shape[2]
    assert ys == 16 and reach <= ys and gx % 2 == 0
    window = 8 * ((ys + 2 * reach + 1 + 7) // 8)
    tiles = rows * nodes * NR // LANES + 1
    f32 = jnp.float32
    vmem = pl.BlockSpec(memory_space=pltpu.VMEM)
    smem = pl.BlockSpec(memory_space=pltpu.SMEM)

    send, deep = pl.pallas_call(
        pack_kernel,
        out_shape=(
            jax.ShapeDtypeStruct((pairs, ys, LANES), f32),
            jax.ShapeDtypeStruct((ys, LANES), f32),
        ),
    )(rhs_conc, rhs_pots, diffusion, exchange, slope)
    own = lax.all_gather(send, "gx", axis=0, tiled=False)
    left = lax.ppermute(own[:, :, ys - reach :], "gy", [(i, i + 1) for i in range(gy - 1)])
    right = lax.ppermute(own[:, :, :reach], "gy", [(i + 1, i) for i in range(gy - 1)])
    spot = lax.axis_index("gx").astype(jnp.int32).reshape(1)

    basis, gram = pl.pallas_call(
        powers_kernel,
        in_specs=[smem] + [vmem] * 6,
        out_specs=(vmem, vmem),
        out_shape=(
            jax.ShapeDtypeStruct((KV, tiles, ys, LANES), f32),
            jax.ShapeDtypeStruct((gx * gy, LANES), f32),
        ),
        scratch_shapes=[
            pltpu.VMEM((FIELDS + 1, gx // 2, window, LANES), f32),
            pltpu.VMEM((ITERS, ys, LANES), f32),
            pltpu.VMEM((tiles - 1, ys, LANES), f32),
            pltpu.VMEM((LANES, 8, LANES), f32),
        ],
    )(spot, rhs_conc, diffusion, own, left, right, deep)

    sums = lax.all_to_all(gram, ("gx", "gy"), 0, 0, tiled=True)

    conc, pots, flag = pl.pallas_call(
        solve_kernel,
        out_shape=(
            jax.ShapeDtypeStruct(rhs_conc.shape, f32),
            jax.ShapeDtypeStruct(rhs_pots.shape, f32),
            jax.ShapeDtypeStruct((1,), jnp.int32),
        ),
        out_specs=(vmem, vmem, smem),
    )(sums, basis)
    return lax.cond(
        flag[0] > 0,
        lambda: plain_cycle(rhs_conc, rhs_pots, diffusion, exchange, slope),
        lambda: (conc, pots),
    )


def solution(mesh):
    spec = P("gx", "gy", None)
    return jax.shard_map(
        shards, mesh=mesh, in_specs=(spec,) * 5, out_specs=(spec, spec), check_vma=False
    )
```

time: 965 us -> 65.7 us (0.07); the launches traced: 951 us -> 65.3 us
  blocking collectives: 457 us -> 11.5 us
  between operations: 171 us -> 1.26 us
  other arithmetic: 118 us -> 0 us
  starting transfers between devices: 104 us -> 11.8 us
  local copies, waits for them, and re-layouts: 87.2 us -> 2.07 us
  Pallas kernels: 0 us -> 21.4 us
    psum x11 -> x0, blocking collectives: 457 us -> none  [the longest x10 415 us: shards(): coeffs, total_square = lax.psum((local_dots, image_square), ('gx', 'gy'))]
    ppermute x40 -> x2, starting transfers between devices: 104 us -> 6 us  [the longest x1 4.57 us: shards(): lax.ppermute(own[:, :, ys - reach:], 'gy', [(i, i + 1) for i in range(gy...]
    div x20 -> x0, other arithmetic: 58.3 us -> none  [the longest x18 58.3 us: shards(): basis.append((rest_conc / height, rest_pots / height))]
    reduce_sum x41 -> x0, other arithmetic: 32.6 us -> none  [the longest x9 11.6 us: shards(): jnp.sum(vector[0] * image_conc) + jnp.sum(vector[1] * image_pots)]
    slice x79 -> x1, local copies, waits for them, and re-layouts: 28.8 us -> 0.06 us  [shards(): own[:, :, :reach]]
    pallas_call x0 -> x3, Pallas kernels: none -> 21.4 us  [the longest x1 12.5 us: shards(): pl.pallas_call(powers_kernel, in_specs=[smem] + [vmem] * 6, out_specs=(vm...]
    concatenate x39 -> x0, other arithmetic: 17.3 us -> none  [the longest x9 9.46 us: mirror_laplace(): outer = jnp.concatenate([values[..., 1:], values[..., -1:]], axis=-1)]
    unnamed x139 -> x14, local copies, waits for them, and re-layouts: 18.5 us -> 2.01 us
  transfers between devices with their start and end apart: 40 -> 3, of which waited for: 10 -> 3; matrix products, arithmetic and copies ran while one was open for 4% -> 0% of each run, Pallas kernels for 0% -> 0%
where the time goes in v1:
time: 65.7 us; the launch traced here: 65.3 us
  Pallas kernels  21.4 us (33%)
  waiting for transfers between devices  17.1 us (26%)
  starting transfers between devices  11.8 us (18%)
  blocking collectives  11.5 us (18%)
  local copies, waits for them, and re-layouts  2.07 us (3%)
  between operations  1.26 us (2%)
    pallas_call x1, Pallas kernels, shards(): pl.pallas_call(powers_kernel, in_specs=[smem] + [vmem] * 6, out_specs=(vm...  12.5 us
    all_gather x1, blocking collectives, shards(): own = lax.all_gather(send, 'gx', axis=0, tiled=False)  11.5 us
    ppermute x1, waiting for transfers between devices, shards(): lax.ppermute(own[:, :, :reach], 'gy', [(i + 1, i) for i in range(gy - 1)])  8.79 us
    all_to_all x1, waiting for transfers between devices, shards(): sums = lax.all_to_all(gram, ('gx', 'gy'), 0, 0, tiled=True)  7.12 us
    all_to_all x1, starting transfers between devices, shards(): sums = lax.all_to_all(gram, ('gx', 'gy'), 0, 0, tiled=True)  5.8 us
    pallas_call x1, Pallas kernels, shards(): pl.pallas_call(solve_kernel, out_shape=(jax.ShapeDtypeStruct(rhs_conc.sha...  5.68 us
    ppermute x1, starting transfers between devices, shards(): lax.ppermute(own[:, :, ys - reach:], 'gy', [(i, i + 1) for i in range(gy...  4.57 us
    pallas_call x1, Pallas kernels, shards(): pl.pallas_call(pack_kernel, out_shape=(jax.ShapeDtypeStruct((pairs, ys, L...  3.28 us
  transfers between devices with their start and end apart: 3, of which 3 were waited for; matrix products, arithmetic and copies ran while one was open for 0% of the time, Pallas kernels for 0%

profile of v1, /device:TPU:0, one launch (start us, length us, event | category | flops | bytes accessed | tf_op | source)
XLA Modules:
  0.0 65.3 jit_solution(12305694572513713806)
XLA Ops:
  0.6 3.3 %shard_map.72 = (f32[7,16,128]{2,1,0:T(8,128)}, f32[16,128]{1,0:T(8,128)}) custom-call(f32[2,16,2048]{2,1,0:T(8,128)} %conc_ref.3, f32[2,16,33]{2,1,0:T(8,128)} %pots_ref.1, f32[2,16,32]{2,1,0:T(8,128)} %diff_ref.3, f32[2,16,32]{2,1,0:T(8,128)} %exch_ref.1, f32[2,16,32]{2,1,0:T(8,128)} %slope_ref.1), custom_call_target="tpu_custom_call" | custom-call | tf_op jit(solution)/shard_map/pallas_call | solution.py:463
  3.9 11.5 %all-gather = f32[56,16,128]{2,1,0:T(8,128)S(1)} all-gather(f32[7,16,128]{2,1,0:T(8,128)} %get-tuple-element.264), channel_id=2, replica_groups=mesh['gx'=8,'gy'=4] {'gx'}, dimensions={0}, use_global_device_ids=true | all-gather | bytes 516096 | tf_op jit(solution)/shard_map/all_gather | solution.py:470
  15.4 0.0 copy-start.6
  15.4 0.0 copy-start.7
  15.4 0.0 copy-start.10
  15.4 0.1 fusion.27
  15.4 1.4 %collective-permute-start.5 = (f32[8,7,10,128]{3,2,1,0:T(8,128)S(1)}, f32[8,7,10,128]{3,2,1,0:T(8,128)S(1)}, u32[]{:S(2)}, u32[]{:S(2)}) collective-permute-start(f32[8,7,10,128]{3,2,1,0:T(8,128)S(1)} %get-tuple-element.328), channel_id=1, source_target_pairs={{1,0},{2,1},{3,2},{5,4},{6,5},{7,6},{9,8},{10,9},{11,10},{13,12},{... | collective-permute-start | bytes 860168 | tf_op jit(solution)/shard_map/ppermute | solution.py:472
  16.9 4.6 %collective-permute-start.4 = (f32[8,7,10,128]{3,2,1,0:T(8,128)S(1)}, f32[8,7,10,128]{3,2,1,0:T(8,128)S(1)}, u32[]{:S(2)}, u32[]{:S(2)}) collective-permute-start(f32[8,7,10,128]{3,2,1,0:T(8,128)S(1)} %get-tuple-element.329), channel_id=1, source_target_pairs={{0,1},{1,2},{2,3},{4,5},{5,6},{6,7},{8,9},{9,10},{10,11},{12,13},{... | collective-permute-start | bytes 860168 | tf_op jit(solution)/shard_map/ppermute | solution.py:471
  21.5 8.8 %collective-permute-done.5.right_ref = f32[8,7,10,128]{3,2,1,0:T(8,128)S(1)} collective-permute-done((f32[8,7,10,128]{3,2,1,0:T(8,128)S(1)}, f32[8,7,10,128]{3,2,1,0:T(8,128)S(1)}, u32[]{:S(2)}, u32[]{:S(2)}) %collective-permute-start.5) | collective-permute-done | bytes 286752 | tf_op jit(solution)/shard_map/ppermute | solution.py:472
  30.2 0.0 copy-start.8
  30.2 1.2 %collective-permute-done.4.left_ref = f32[8,7,10,128]{3,2,1,0:T(8,128)S(1)} collective-permute-done((f32[8,7,10,128]{3,2,1,0:T(8,128)S(1)}, f32[8,7,10,128]{3,2,1,0:T(8,128)S(1)}, u32[]{:S(2)}, u32[]{:S(2)}) %collective-permute-start.4) | collective-permute-done | bytes 286752 | tf_op jit(solution)/shard_map/ppermute | solution.py:471
  31.4 0.0 copy-start.9
  31.4 0.0 copy-done.6
  31.4 0.0 copy-done.8
  31.4 0.8 %copy-done.9 = f32[8,7,10,128]{3,2,1,0:T(8,128)} copy-done((f32[8,7,10,128]{3,2,1,0:T(8,128)}, f32[8,7,10,128]{3,2,1,0:T(8,128)S(1)}, u32[]{:S(2)}) %copy-start.9) | copy-done | bytes 286744
  32.2 12.5 %shard_map.73 = (f32[11,33,16,128]{3,2,1,0:T(8,128)}, f32[32,128]{1,0:T(8,128)}) custom-call(s32[1]{0:T(128)} %bitcast.3.spot_ref, f32[2,16,2048]{2,1,0:T(8,128)} %conc_ref.3, f32[2,16,32]{2,1,0:T(8,128)} %diff_ref.3, f32[8,7,16,128]{3,2,1,0:T(8,128)} %bitcast.92, f32[8,7,10,128]{3,2,1,0:T(8,128)} %copy-done.9, f32[8,7,10,128]{3,2,1,0:T(8,128)} %copy-done.8, ...), custom_call_target="tpu_custom_call" | custom-call | tf_op jit(solution)/shard_map/pallas_call | solution.py:475
  44.7 5.8 %all-to-all-start = ((f32[32,1,128]{2,1,0:T(1,128)}), f32[32,1,128]{2,1,0:T(1,128)S(1)}, u32[]{:S(2)}, u32[]{:S(2)}) async-start(f32[32,1,128]{2,1,0:T(1,128)} %bitcast.96), calls=%async_computation | async-start | bytes 32768 | tf_op jit(solution)/shard_map/all_to_all | solution.py:491
  50.5 7.1 %all-to-all-done = f32[32,1,128]{2,1,0:T(1,128)S(1)} async-done(((f32[32,1,128]{2,1,0:T(1,128)}), f32[32,1,128]{2,1,0:T(1,128)S(1)}, u32[]{:S(2)}, u32[]{:S(2)}) %all-to-all-start) | async-done | bytes 16416 | tf_op jit(solution)/shard_map/all_to_all | solution.py:491
  57.6 0.0 copy-start.11
  57.6 0.6 copy-done.11
  58.2 5.7 %shard_map.74 = (f32[2,16,2048]{2,1,0:T(8,128)}, f32[2,16,33]{2,1,0:T(8,128)S(1)}, s32[1]{0:T(128)}) custom-call(f32[32,128]{1,0:T(8,128)} %bitcast.95, f32[11,33,16,128]{3,2,1,0:T(8,128)} %get-tuple-element.267.basis_ref), custom_call_target="tpu_custom_call" | custom-call | tf_op jit(solution)/shard_map/pallas_call | solution.py:493
  64.5 0.0 copy-done.7
  64.5 0.0 copy-done.10
  64.5 0.2 conditional.1
  64.7 0.0 copy-start.12
  64.7 0.6 copy-done.12
Async XLA Ops:
  15.4 16.1 %copy-start.6 = (f32[56,16,128]{2,1,0:T(8,128)}, f32[56,16,128]{2,1,0:T(8,128)S(1)}, u32[]{:S(2)}) copy-start(f32[56,16,128]{2,1,0:T(8,128)S(1)} %all-gather) | copy-start | bytes 1376260
  15.4 49.1 %copy-start.7 = (f32[2,16,2048]{2,1,0:T(8,128)S(1)}, f32[2,16,2048]{2,1,0:T(8,128)}, u32[]{:S(2)}) copy-start(f32[2,16,2048]{2,1,0:T(8,128)} %conc_ref.3) | copy-start | bytes 786436
  15.4 49.1 %copy-start.10 = (f32[2,16,33]{2,1,0:T(8,128)S(1)}, f32[2,16,33]{2,1,0:T(8,128)}, u32[]{:S(2)}) copy-start(f32[2,16,33]{2,1,0:T(8,128)} %pots_ref.1) | copy-start | bytes 12676
  15.4 14.8 %collective-permute-start.5 = (f32[8,7,10,128]{3,2,1,0:T(8,128)S(1)}, f32[8,7,10,128]{3,2,1,0:T(8,128)S(1)}, u32[]{:S(2)}, u32[]{:S(2)}) collective-permute-start(f32[8,7,10,128]{3,2,1,0:T(8,128)S(1)} %get-tuple-element.328), channel_id=1, source_target_pairs={{1,0},{2,1},{3,2},{5,4},{6,5},{7,6},{9,8},{10,9},{11,10},{13,12},{... | collective-permute-start | bytes 860168 | tf_op jit(solution)/shard_map/ppermute | solution.py:472
  16.9 14.6 %collective-permute-start.4 = (f32[8,7,10,128]{3,2,1,0:T(8,128)S(1)}, f32[8,7,10,128]{3,2,1,0:T(8,128)S(1)}, u32[]{:S(2)}, u32[]{:S(2)}) collective-permute-start(f32[8,7,10,128]{3,2,1,0:T(8,128)S(1)} %get-tuple-element.329), channel_id=1, source_target_pairs={{0,1},{1,2},{2,3},{4,5},{5,6},{6,7},{8,9},{9,10},{10,11},{12,13},{... | collective-permute-start | bytes 860168 | tf_op jit(solution)/shard_map/ppermute | solution.py:471
  30.2 1.2 %copy-start.8 = (f32[8,7,10,128]{3,2,1,0:T(8,128)}, f32[8,7,10,128]{3,2,1,0:T(8,128)S(1)}, u32[]{:S(2)}) copy-start(f32[8,7,10,128]{3,2,1,0:T(8,128)S(1)} %collective-permute-done.5.right_ref) | copy-start | bytes 860164
  31.4 0.8 %copy-start.9 = (f32[8,7,10,128]{3,2,1,0:T(8,128)}, f32[8,7,10,128]{3,2,1,0:T(8,128)S(1)}, u32[]{:S(2)}) copy-start(f32[8,7,10,128]{3,2,1,0:T(8,128)S(1)} %collective-permute-done.4.left_ref) | copy-start | bytes 860164
  44.7 12.9 %all-to-all-start = ((f32[32,1,128]{2,1,0:T(1,128)}), f32[32,1,128]{2,1,0:T(1,128)S(1)}, u32[]{:S(2)}, u32[]{:S(2)}) async-start(f32[32,1,128]{2,1,0:T(1,128)} %bitcast.96), calls=%async_computation | async-start | bytes 32768 | tf_op jit(solution)/shard_map/all_to_all | solution.py:491
  57.6 0.6 copy-start.11
  64.7 0.6 copy-start.12

commit v2 on v1

--- a/solution.py
+++ b/solution.py
@@ -25,6 +25,9 @@
 PAIRS = KV * (KV + 1) // 2
 SHELLS = ITERS - 1
 FIELDS = 5 + SHELLS
+REACHES = [ITERS, SHELLS, SHELLS] + [SHELLS - k for k in range(1, SHELLS, 2)]
+STARTS = [sum(REACHES[:pair]) for pair in range(len(REACHES))]
+EDGE = sum(REACHES)
 
 
 def lanes_of(shape):
@@ -35,7 +38,7 @@
     return jnp.take_along_axis(values, index, axis=1, mode="promise_in_bounds")
 
 
-def pack_kernel(conc_ref, pots_ref, diff_ref, exch_ref, slope_ref, send_ref, deep_ref):
+def pack_kernel(conc_ref, pots_ref, diff_ref, exch_ref, slope_ref, send_ref, up_ref, down_ref, deep_ref):
     rows, ys, nodes = exch_ref.shape
     half = rows * nodes
     lane = lanes_of((ys, LANES))
@@ -58,23 +61,27 @@
                 found = pick(cells, (node % 2) * NR + (NR - 1 - k))
                 shells[k] = jnp.where(here, found, shells[k])
     low = lane < half
-    send_ref[0] = jnp.concatenate([plain[0], plain[1]], axis=1)
-    send_ref[1] = jnp.concatenate([plain[2], plain[3]], axis=1)
-    send_ref[2] = jnp.where(low, jnp.concatenate([plain[4], plain[4]], axis=1), shells[0])
-    for k in range(1, SHELLS, 2):
-        send_ref[2 + (k + 1) // 2] = jnp.where(low, shells[k], shells[k + 1])
+    packed = [
+        jnp.concatenate([plain[0], plain[1]], axis=1),
+        jnp.concatenate([plain[2], plain[3]], axis=1),
+        jnp.where(low, jnp.concatenate([plain[4], plain[4]], axis=1), shells[0]),
+    ]
+    packed += [jnp.where(low, shells[k], shells[k + 1]) for k in range(1, SHELLS, 2)]
+    for pair, (value, reach, start) in enumerate(zip(packed, REACHES, STARTS)):
+        send_ref[pair * ys : (pair + 1) * ys, :] = value
+        up_ref[start : start + reach, :] = value[ys - reach :]
+        down_ref[start : start + reach, :] = value[:reach]
     deep_ref[...] = shells[SHELLS]
 
 
 def powers_kernel(
-    spot_ref, conc_ref, diff_ref, own_ref, left_ref, right_ref, deep_ref,
+    spot_ref, conc_ref, diff_ref, all_ref, deep_ref,
     basis_ref, gram_ref,
     field_ref, current_ref, dexp_ref, acc_ref,
 ):
     rows, ys, nodes = diff_ref.shape
-    blocks = own_ref.shape[0]
+    blocks = all_ref.shape[0]
     half = rows * nodes
-    reach = left_ref.shape[2]
     quads = blocks // 2
     window = field_ref.shape[2]
     spot = spot_ref[0]
@@ -83,17 +90,24 @@
     lane2 = lanes_of((ys, LANES))
 
     field_ref[...] = jnp.zeros(field_ref.shape, jnp.float32)
-    for source, start, count in ((own_ref, 0, ys), (right_ref, ys, reach), (left_ref, window - reach, reach)):
-        low = lanes_of((count, LANES)) < half
-        for field in range(FIELDS):
+    body = (FIELDS // 2) * ys
+    for field in range(FIELDS):
+        pair = field // 2
+        reach, start = REACHES[pair], STARTS[pair]
+        for place, origin, count in (
+            (0, pair * ys, ys),
+            (window - reach, body + start, reach),
+            (ys, body + EDGE + start, reach),
+        ):
+            low = lanes_of((count, LANES)) < half
             for q in range(quads):
-                a = source[2 * q, field // 2]
-                b = source[2 * q + 1, field // 2]
+                a = all_ref[2 * q, origin : origin + count, :]
+                b = all_ref[2 * q + 1, origin : origin + count, :]
                 if field % 2 == 0:
                     value = jnp.where(low, a, pltpu.roll(b, half, 1))
                 else:
                     value = jnp.where(low, pltpu.roll(a, half, 1), b)
-                field_ref[field, q, start : start + count, :] = value
+                field_ref[field, q, place : place + count, :] = value
     field_ref[FIELDS, quad, 0:ys, :] = deep_ref[...]
 
     shape = (quads, window, LANES)
@@ -451,31 +465,36 @@
     gx, gy = lax.axis_size("gx"), lax.axis_size("gy")
     half = rows * nodes
     pairs = FIELDS // 2
-    reach = ITERS
     assert half * 2 == LANES and nodes * NR == rhs_conc.shape[2]
-    assert ys == 16 and reach <= ys and gx % 2 == 0
-    window = 8 * ((ys + 2 * reach + 1 + 7) // 8)
+    assert ys == 16 and ITERS <= ys and gx % 2 == 0
+    window = 8 * ((ys + 2 * ITERS + 1 + 7) // 8)
     tiles = rows * nodes * NR // LANES + 1
     f32 = jnp.float32
     vmem = pl.BlockSpec(memory_space=pltpu.VMEM)
     smem = pl.BlockSpec(memory_space=pltpu.SMEM)
-
-    send, deep = pl.pallas_call(
+    params = pltpu.CompilerParams(vmem_limit_bytes=24 << 20)
+
+    send, up, down, deep = pl.pallas_call(
         pack_kernel,
         out_shape=(
-            jax.ShapeDtypeStruct((pairs, ys, LANES), f32),
+            jax.ShapeDtypeStruct((pairs * ys, LANES), f32),
+            jax.ShapeDtypeStruct((EDGE, LANES), f32),
+            jax.ShapeDtypeStruct((EDGE, LANES), f32),
             jax.ShapeDtypeStruct((ys, LANES), f32),
         ),
+        compiler_params=params,
     )(rhs_conc, rhs_pots, diffusion, exchange, slope)
-    own = lax.all_gather(send, "gx", axis=0, tiled=False)
-    left = lax.ppermute(own[:, :, ys - reach :], "gy", [(i, i + 1) for i in range(gy - 1)])
-    right = lax.ppermute(own[:, :, :reach], "gy", [(i + 1, i) for i in range(gy - 1)])
+    left = lax.ppermute(up, "gy", [(i, i + 1) for i in range(gy - 1)])
+    right = lax.ppermute(down, "gy", [(i + 1, i) for i in range(gy - 1)])
+    block = jnp.concatenate([send, left, right], axis=0)
+    everything = lax.all_gather(block, "gx", axis=0, tiled=False)
     spot = lax.axis_index("gx").astype(jnp.int32).reshape(1)
 
     basis, gram = pl.pallas_call(
         powers_kernel,
-        in_specs=[smem] + [vmem] * 6,
+        in_specs=[smem] + [vmem] * 4,
         out_specs=(vmem, vmem),
+        compiler_params=params,
         out_shape=(
             jax.ShapeDtypeStruct((KV, tiles, ys, LANES), f32),
             jax.ShapeDtypeStruct((gx * gy, LANES), f32),
@@ -486,7 +505,7 @@
             pltpu.VMEM((tiles - 1, ys, LANES), f32),
             pltpu.VMEM((LANES, 8, LANES), f32),
         ],
-    )(spot, rhs_conc, diffusion, own, left, right, deep)
+    )(spot, rhs_conc, diffusion, everything, deep)
 
     sums = lax.all_to_all(gram, ("gx", "gy"), 0, 0, tiled=True)
 
@@ -498,6 +517,7 @@
             jax.ShapeDtypeStruct((1,), jnp.int32),
         ),
         out_specs=(vmem, vmem, smem),
+        compiler_params=params,
     )(sums, basis)
     return lax.cond(
         flag[0] > 0,

time: 65.7 us -> 52.9 us (0.81)
  waiting for transfers between devices: 17.1 us -> 11.5 us
  Pallas kernels: 21.4 us -> 17.5 us
  starting transfers between devices: 11.8 us -> 10.1 us
  blocking collectives: 11.5 us -> 10.5 us
  local copies, waits for them, and re-layouts: 2.07 us -> 1.31 us
    ppermute x2, waiting for transfers between devices: 9.97 us -> 4.42 us  [the longest x1 4.22 us: shards(): right = lax.ppermute(down, 'gy', [(i + 1, i) for i in range(gy - 1)])]
    pallas_call x1, Pallas kernels: 5.68 us -> 3.46 us  [shards(): pl.pallas_call(solve_kernel, out_shape=(jax.ShapeDtypeStruct(rhs_conc.sha...]
    all_to_all x1, starting transfers between devices: 5.8 us -> 3.89 us  [shards(): sums = lax.all_to_all(gram, ('gx', 'gy'), 0, 0, tiled=True)]
    pallas_call x2, Pallas kernels: 15.8 us -> 14 us  [the longest x1 11.3 us: shards(): pl.pallas_call(powers_kernel, in_specs=[smem] + [vmem] * 4, out_specs=(vm...]
    all_gather x1, blocking collectives: 11.5 us -> 10.5 us  [shards(): everything = lax.all_gather(block, 'gx', axis=0, tiled=False)]
    unnamed x14 -> x8, local copies, waits for them, and re-layouts: 2.01 us -> 1.31 us
where the time goes in v2:
time: 52.9 us; the launch traced here: 52.6 us
  Pallas kernels  17.5 us (33%)
  waiting for transfers between devices  11.5 us (22%)
  blocking collectives  10.5 us (20%)
  starting transfers between devices  10.1 us (19%)
  between operations  1.38 us (3%)
  local copies, waits for them, and re-layouts  1.31 us (2%)
    pallas_call x1, Pallas kernels, shards(): pl.pallas_call(powers_kernel, in_specs=[smem] + [vmem] * 4, out_specs=(vm...  11.3 us
    all_gather x1, blocking collectives, shards(): everything = lax.all_gather(block, 'gx', axis=0, tiled=False)  10.5 us
    all_to_all x1, waiting for transfers between devices, shards(): sums = lax.all_to_all(gram, ('gx', 'gy'), 0, 0, tiled=True)  7.12 us
    ppermute x1, starting transfers between devices, shards(): left = lax.ppermute(up, 'gy', [(i, i + 1) for i in range(gy - 1)])  4.96 us
    ppermute x1, waiting for transfers between devices, shards(): right = lax.ppermute(down, 'gy', [(i + 1, i) for i in range(gy - 1)])  4.22 us
    all_to_all x1, starting transfers between devices, shards(): sums = lax.all_to_all(gram, ('gx', 'gy'), 0, 0, tiled=True)  3.89 us
    pallas_call x1, Pallas kernels, shards(): pl.pallas_call(solve_kernel, out_shape=(jax.ShapeDtypeStruct(rhs_conc.sha...  3.46 us
    pallas_call x1, Pallas kernels, shards(): pl.pallas_call(pack_kernel, out_shape=(jax.ShapeDtypeStruct((pairs * ys,...  2.69 us
  transfers between devices with their start and end apart: 3, of which 3 were waited for; matrix products, arithmetic and copies ran while one was open for 0% of the time, Pallas kernels for 0%

profile of v2, /device:TPU:0, one launch (start us, length us, event | category | flops | bytes accessed | tf_op | source)
XLA Modules:
  0.0 52.6 jit_solution(13131276416722955699)
XLA Ops:
  0.6 0.0 copy-start.6
  0.6 0.0 copy-start.7
  0.7 2.7 %shard_map.72 = (f32[112,128]{1,0:T(8,128)S(1)}, f32[48,128]{1,0:T(8,128)S(1)}, f32[48,128]{1,0:T(8,128)S(1)}, f32[16,128]{1,0:T(8,128)S(1)}) custom-call(f32[2,16,2048]{2,1,0:T(8,128)} %conc_ref.3, f32[2,16,33]{2,1,0:T(8,128)} %pots_ref.1, f32[2,16,32]{2,1,0:T(8,128)} %diff_ref.3, f32[2,16,32]{2,1,0:T(8,128)} %exch_ref.1, f32[2,16,32]{2,1,0:T(8,128)} %slope_ref.1), custom_call_target="tpu_custom_call" | custom-call | tf_op jit(solution)/shard_map/pallas_call | solution.py:477
  3.4 5.0 %collective-permute-start.4 = (f32[48,128]{1,0:T(8,128)S(1)}, f32[48,128]{1,0:T(8,128)S(1)}, u32[]{:S(2)}, u32[]{:S(2)}) collective-permute-start(f32[48,128]{1,0:T(8,128)S(1)} %get-tuple-element.267), channel_id=1, source_target_pairs={{0,1},{1,2},{2,3},{4,5},{5,6},{6,7},{8,9},{9,10},{10,11},{12,13},{... | collective-permute-start | bytes 73736 | tf_op jit(solution)/shard_map/ppermute | solution.py:487
  8.3 1.3 %collective-permute-start.5 = (f32[48,128]{1,0:T(8,128)S(1)}, f32[48,128]{1,0:T(8,128)S(1)}, u32[]{:S(2)}, u32[]{:S(2)}) collective-permute-start(f32[48,128]{1,0:T(8,128)S(1)} %get-tuple-element.268), channel_id=1, source_target_pairs={{1,0},{2,1},{3,2},{5,4},{6,5},{7,6},{9,8},{10,9},{11,10},{13,12},{... | collective-permute-start | bytes 73736 | tf_op jit(solution)/shard_map/ppermute | solution.py:488
  9.6 0.2 collective-permute-done.4
  9.8 4.2 %collective-permute-done.5 = f32[48,128]{1,0:T(8,128)S(1)} collective-permute-done((f32[48,128]{1,0:T(8,128)S(1)}, f32[48,128]{1,0:T(8,128)S(1)}, u32[]{:S(2)}, u32[]{:S(2)}) %collective-permute-start.5) | collective-permute-done | bytes 24608 | tf_op jit(solution)/shard_map/ppermute | solution.py:488
  14.1 10.5 %all-gather = f32[1664,128]{1,0:T(8,128)S(1)} all-gather(f32[208,128]{1,0:T(8,128)S(1)} %pad_maximum_fusion.7), channel_id=2, replica_groups=mesh['gx'=8,'gy'=4] {'gx'}, dimensions={0}, use_global_device_ids=true | all-gather | bytes 958464 | tf_op jit(solution)/shard_map/all_gather | solution.py:490
  24.6 11.3 %shard_map.73 = (f32[11,33,16,128]{3,2,1,0:T(8,128)S(1)}, f32[32,128]{1,0:T(8,128)}) custom-call(s32[1]{0:T(128)} %bitcast.3.spot_ref, f32[2,16,2048]{2,1,0:T(8,128)} %conc_ref.3, f32[2,16,32]{2,1,0:T(8,128)} %diff_ref.3, f32[8,208,128]{2,1,0:T(8,128)S(1)} %bitcast.90, f32[16,128]{1,0:T(8,128)S(1)} %get-tuple-element.269.deep_ref), custom_call_target="tpu_custom_call" | custom-call | tf_op jit(solution)/shard_map/pallas_call | solution.py:493
  35.9 3.9 %all-to-all-start = ((f32[32,1,128]{2,1,0:T(1,128)}), f32[32,1,128]{2,1,0:T(1,128)S(1)}, u32[]{:S(2)}, u32[]{:S(2)}) async-start(f32[32,1,128]{2,1,0:T(1,128)} %bitcast.6), calls=%async_computation | async-start | bytes 32768 | tf_op jit(solution)/shard_map/all_to_all | solution.py:510
  39.8 7.1 %all-to-all-done = f32[32,1,128]{2,1,0:T(1,128)S(1)} async-done(((f32[32,1,128]{2,1,0:T(1,128)}), f32[32,1,128]{2,1,0:T(1,128)S(1)}, u32[]{:S(2)}, u32[]{:S(2)}) %all-to-all-start) | async-done | bytes 16416 | tf_op jit(solution)/shard_map/all_to_all | solution.py:510
  46.9 3.5 %shard_map.74 = (f32[2,16,2048]{2,1,0:T(8,128)S(1)}, f32[2,16,33]{2,1,0:T(8,128)S(1)}, s32[1]{0:T(128)}) custom-call(f32[32,128]{1,0:T(8,128)S(1)} %bitcast.91, f32[11,33,16,128]{3,2,1,0:T(8,128)S(1)} %get-tuple-element.271.basis_ref), custom_call_target="tpu_custom_call" | custom-call | tf_op jit(solution)/shard_map/pallas_call | solution.py:512
  51.1 0.0 copy-done.6
  51.1 0.0 copy-done.7
  51.1 0.2 conditional.1
  51.3 0.0 copy-start.8
  51.3 0.7 %copy-done.8 = f32[2,16,2048]{2,1,0:T(8,128)} copy-done((f32[2,16,2048]{2,1,0:T(8,128)}, f32[2,16,2048]{2,1,0:T(8,128)S(1)}, u32[]{:S(2)}) %copy-start.8) | copy-done | bytes 262168
  52.0 0.0 copy-start.9
  52.0 0.6 %copy-done.9 = f32[2,16,33]{2,1,0:T(8,128)} copy-done((f32[2,16,33]{2,1,0:T(8,128)}, f32[2,16,33]{2,1,0:T(8,128)S(1)}, u32[]{:S(2)}) %copy-start.9) | copy-done | bytes 4248
  (1 shorter events, 0.0 us)
Async XLA Ops:
  0.6 50.4 %copy-start.6 = (f32[2,16,2048]{2,1,0:T(8,128)S(1)}, f32[2,16,2048]{2,1,0:T(8,128)}, u32[]{:S(2)}) copy-start(f32[2,16,2048]{2,1,0:T(8,128)} %conc_ref.3) | copy-start | bytes 786436
  0.6 50.4 %copy-start.7 = (f32[2,16,33]{2,1,0:T(8,128)S(1)}, f32[2,16,33]{2,1,0:T(8,128)}, u32[]{:S(2)}) copy-start(f32[2,16,33]{2,1,0:T(8,128)} %pots_ref.1) | copy-start | bytes 12676
  3.4 6.5 %collective-permute-start.4 = (f32[48,128]{1,0:T(8,128)S(1)}, f32[48,128]{1,0:T(8,128)S(1)}, u32[]{:S(2)}, u32[]{:S(2)}) collective-permute-start(f32[48,128]{1,0:T(8,128)S(1)} %get-tuple-element.267), channel_id=1, source_target_pairs={{0,1},{1,2},{2,3},{4,5},{5,6},{6,7},{8,9},{9,10},{10,11},{12,13},{... | collective-permute-start | bytes 73736 | tf_op jit(solution)/shard_map/ppermute | solution.py:487
  8.3 5.7 %collective-permute-start.5 = (f32[48,128]{1,0:T(8,128)S(1)}, f32[48,128]{1,0:T(8,128)S(1)}, u32[]{:S(2)}, u32[]{:S(2)}) collective-permute-start(f32[48,128]{1,0:T(8,128)S(1)} %get-tuple-element.268), channel_id=1, source_target_pairs={{1,0},{2,1},{3,2},{5,4},{6,5},{7,6},{9,8},{10,9},{11,10},{13,12},{... | collective-permute-start | bytes 73736 | tf_op jit(solution)/shard_map/ppermute | solution.py:488
  35.9 11.0 %all-to-all-start = ((f32[32,1,128]{2,1,0:T(1,128)}), f32[32,1,128]{2,1,0:T(1,128)S(1)}, u32[]{:S(2)}, u32[]{:S(2)}) async-start(f32[32,1,128]{2,1,0:T(1,128)} %bitcast.6), calls=%async_computation | async-start | bytes 32768 | tf_op jit(solution)/shard_map/all_to_all | solution.py:510
  51.3 0.7 %copy-start.8 = (f32[2,16,2048]{2,1,0:T(8,128)}, f32[2,16,2048]{2,1,0:T(8,128)S(1)}, u32[]{:S(2)}) copy-start(f32[2,16,2048]{2,1,0:T(8,128)S(1)} %get-tuple-element.465) | copy-start | bytes 786436
  52.0 0.6 %copy-start.9 = (f32[2,16,33]{2,1,0:T(8,128)}, f32[2,16,33]{2,1,0:T(8,128)S(1)}, u32[]{:S(2)}) copy-start(f32[2,16,33]{2,1,0:T(8,128)S(1)} %get-tuple-element.467) | copy-start | bytes 12676

commit v3 on v2

v3 whole, which is shorter than its diff:
```python
import functools

import jax
import jax.numpy as jnp
from jax import lax
from jax.experimental import pallas as pl
from jax.experimental.pallas import tpu as pltpu
from jax.sharding import PartitionSpec as P

ITERS = 10
NR = 64
LANES = 128

node_cond = 1.0
plane_cond = 0.5
collector_cond = 2.0
epsilon = 1e-06

CENTER = 10.45
HALF = 9.55
INVERSE_MAX = 2.0e3
NORM_MIN = 1.0

KV = ITERS + 1
PAIRS = KV * (KV + 1) // 2
SHELLS = ITERS - 1
FIELDS = 5 + SHELLS
REACHES = [ITERS, SHELLS, SHELLS] + [SHELLS - k for k in range(1, SHELLS, 2)]
STARTS = [sum(REACHES[:pair]) for pair in range(len(REACHES))]
EDGE = sum(REACHES)


def lanes_of(shape):
    return lax.broadcasted_iota(jnp.int32, shape, len(shape) - 1)


def pick(values, index):
    return jnp.take_along_axis(values, index, axis=1, mode="promise_in_bounds")


def pack_kernel(conc_ref, pots_ref, diff_ref, exch_ref, slope_ref, send_ref, up_ref, down_ref):
    rows, ys, nodes = exch_ref.shape
    half = rows * nodes
    lane = lanes_of((ys, LANES))
    low = lane < half

    def join(ref):
        return [ref[x][:, :nodes] for x in range(rows)]

    collector = [
        jnp.broadcast_to(pots_ref[x][:, nodes : nodes + 1], (ys, nodes)) for x in range(rows)
    ]
    slope = join(slope_ref)
    packed = [
        jnp.concatenate(join(pots_ref) + collector, axis=1),
        jnp.concatenate(join(diff_ref) + join(exch_ref), axis=1),
        jnp.where(low, jnp.concatenate(slope + slope, axis=1), outer_shells(conc_ref, nodes, 0, 0)),
    ]
    packed += [outer_shells(conc_ref, nodes, k, k + 1) for k in range(1, SHELLS, 2)]
    for pair, (value, reach, start) in enumerate(zip(packed, REACHES, STARTS)):
        send_ref[pair * ys : (pair + 1) * ys, :] = value
        up_ref[start : start + reach, :] = value[ys - reach :]
        down_ref[start : start + reach, :] = value[:reach]


def outer_shells(conc_ref, nodes, near, far):
    rows, ys, width = conc_ref.shape
    half = rows * nodes
    lane = lanes_of((ys, LANES))
    node = lane % half
    index = (node % 2) * NR + (NR - 1 - near) - jnp.where(lane < half, 0, far - near)
    found = jnp.zeros((ys, LANES), jnp.float32)
    for x in range(rows):
        for tile in range(width // LANES):
            cells = conc_ref[x, :, tile * LANES : (tile + 1) * LANES]
            here = (node // 2) == (x * nodes // 2 + tile)
            found = jnp.where(here, pick(cells, index), found)
    return found


GAIN = 2.0 / HALF
KEEP = GAIN * (1.0 - CENTER)


def add_gram(cells, lead_mask, acc_ref):
    pair = 0
    for i in range(KV):
        lead = cells[i] if lead_mask is None else cells[i] * lead_mask
        for j in range(i, KV):
            product = lead * cells[j]
            if product.shape[0] == 16:
                product = product[:8] + product[8:]
            acc_ref[pair] += product
            pair += 1


def lane_totals(acc_ref, count):
    sums = jnp.sum(acc_ref[...], axis=1)
    return lax.dot_general(
        jnp.ones((count, LANES), jnp.float32), sums, (((1,), (1,)), ((), ())),
        precision=lax.Precision.HIGHEST, preferred_element_type=jnp.float32,
    )


def turn_nodes(turned, at, rows, ys, nodes):
    lane = lanes_of((8, LANES))
    result = jnp.zeros((8, LANES), jnp.float32)
    for slot in range(nodes // 8):
        for x in range(rows):
            start = x * nodes + 8 * slot
            place = (slot * rows + x) * ys
            piece = pltpu.roll(turned[start : start + 8, :], (place - at) % LANES, 1)
            result = jnp.where((lane >= place) & (lane < place + ys), piece, result)
    return result


def free_kernel(conc_ref, diff_ref, basis_ref, coef_ref, deep_ref, gram_ref, last_ref, acc_ref):
    rows, ys, nodes = diff_ref.shape
    slots = nodes // 8
    deep_ref[...] = outer_shells(conc_ref, nodes, SHELLS, SHELLS)
    spread = jnp.concatenate([diff_ref[x] for x in range(rows)] * 2, axis=1)
    spread = jnp.concatenate([spread] * (LANES // ys), axis=0)
    gain = GAIN * turn_nodes(spread.T, 0, rows, ys, nodes)
    coef_ref[0] = gain
    coef_ref[1] = KEEP + 2.0 * gain
    for group in range(4):
        cells = jnp.concatenate(
            [
                conc_ref[x, :, (4 * slot + group) * LANES : (4 * slot + group + 1) * LANES]
                for slot in range(slots)
                for x in range(rows)
            ],
            axis=0,
        ).T
        for upper in range(LANES // NR):
            basis_ref[0, 2 * group + upper] = cells[upper * NR : (upper + 1) * NR]
    sub = lax.broadcasted_iota(jnp.int32, (8, LANES), 0)

    def image(step, row, base):
        now = basis_ref[step, row, base : base + 8, :]
        if base == 0:
            prev = jnp.where(sub == 0, now, pltpu.roll(now, 1, 0))
        else:
            prev = basis_ref[step, row, base - 1 : base + 7, :]
        if base == NR - 8:
            following = jnp.where(sub == 7, now, pltpu.roll(now, 7, 0))
        else:
            following = basis_ref[step, row, base + 1 : base + 9, :]
        gain = jnp.broadcast_to(coef_ref[0, row : row + 1, :], (8, LANES))
        keep = jnp.broadcast_to(coef_ref[1, row : row + 1, :], (8, LANES))
        return keep * now - gain * (prev + following)

    for row in range(8):
        for base in range(0, NR, 8):
            basis_ref[1, row, base : base + 8, :] = 0.5 * image(0, row, base)

    def advance(step, carry):
        for row in range(8):
            for base in range(0, NR, 8):
                basis_ref[step + 1, row, base : base + 8, :] = (
                    image(step, row, base) - basis_ref[step - 1, row, base : base + 8, :]
                )
        return carry

    lax.fori_loop(1, ITERS - 1, advance, 0)
    for row in range(8):
        for base in range(0, NR, 8):
            last_ref[row, base : base + 8, :] = (
                image(ITERS - 1, row, base) - basis_ref[ITERS - 2, row, base : base + 8, :]
            )

    def cells(row, start, stop):
        line = [basis_ref[k, row, start:stop, :] for k in range(ITERS)]
        return line + [last_ref[row, start:stop, :]]

    acc_ref[...] = jnp.zeros(acc_ref.shape, jnp.float32)
    inner = jnp.where(sub < 16 - ITERS, 1.0, 0.0)

    def gram_row(row, carry):
        for base in range(0, NR - 16, 16):
            add_gram(cells(row, base, base + 16), None, acc_ref)
        add_gram(cells(row, NR - 16, NR - 8), inner, acc_ref)
        return carry

    lax.fori_loop(0, 8, gram_row, 0)
    gram_ref[...] = lane_totals(acc_ref, 8)


def powers_kernel(
    spot_ref, all_ref, basis_ref, coeft_ref, deep_ref, inner_ref,
    outer_ref, gram_ref,
    pot_ref, col_ref, shell_ref, coef_ref, flow_ref, mean_ref, own_ref, tail_ref, acc_ref,
    *, rows, nodes,
):
    ys = deep_ref.shape[0]
    half = rows * nodes
    quads = all_ref.shape[0] // 2
    window = pot_ref.shape[2]
    spot = spot_ref[0]
    quad = spot // 2
    odd = (spot % 2) == 1
    lane2 = lanes_of((ys, LANES))
    low2 = lane2 < half
    head = (lane2 % nodes) == 0

    def room(field):
        if field < 2:
            return (pot_ref if field == 0 else col_ref).at[0]
        return coef_ref.at[field - 2] if field < 5 else shell_ref.at[0, field - 5]

    body = (FIELDS // 2) * ys
    for field in range(FIELDS):
        pair = field // 2
        reach, start = REACHES[pair], STARTS[pair]
        gap = (ys + reach, window - reach)
        scale = GAIN if field == 2 else 1.0
        for q in range(quads):
            room(field)[q, gap[0] : gap[1], :] = jnp.zeros((gap[1] - gap[0], LANES), jnp.float32)
            for place, origin, count in (
                (0, pair * ys, ys),
                (window - reach, body + start, reach),
                (ys, body + EDGE + start, reach),
            ):
                low = lanes_of((count, LANES)) < half
                a = all_ref[2 * q, origin : origin + count, :]
                b = all_ref[2 * q + 1, origin : origin + count, :]
                if field % 2 == 0:
                    value = jnp.where(low, a, pltpu.roll(b, half, 1))
                else:
                    value = jnp.where(low, pltpu.roll(a, half, 1), b)
                room(field)[q, place : place + count, :] = value * scale if field == 2 else value
    for q in range(quads):
        shell_ref[0, SHELLS, q] = jnp.zeros((window, LANES), jnp.float32)
    shell_ref[0, SHELLS, quad, 0:ys, :] = deep_ref[...]

    block = (lax.broadcasted_iota(jnp.int32, (LANES, LANES), 0) // nodes) == (
        lanes_of((LANES, LANES)) // nodes
    )
    mean_mat = jnp.where(block, 1.0 / nodes, 0.0).astype(jnp.bfloat16)
    def own_of(value):
        return jnp.where(odd, pltpu.roll(value, half, 1), value)

    def room_for(step):
        return outer_ref.at[step] if step < ITERS else tail_ref

    for step in range(KV):
        now, old = step % 2, (step + 1) % 2
        own_p = own_of(pot_ref[now, quad, 0:ys, :])
        own_v = own_of(col_ref[now, quad, 0:ys, :])
        room_for(step)[8] = jnp.where(
            low2, own_p, jnp.where(head, pltpu.roll(own_v, half, 1), 0.0)
        )
        if step == ITERS:
            break
        spans = [(0, window)] if step < 2 else [(0, ys + 8), (window - 8, window)]
        size = sum(stop - start for start, stop in spans)
        lane = lanes_of((size, LANES))

        def load(view):
            return jnp.concatenate([view[start:stop, :] for start, stop in spans], axis=0)

        def store(view, value):
            at = 0
            for start, stop in spans:
                view[start:stop, :] = value[at : at + stop - start]
                at += stop - start

        def around(ref, q):
            here = load(ref.at[now, q])
            following = load(ref.at[now, q + 1]) if q + 1 < quads else jnp.zeros_like(here)
            previous = load(ref.at[now, q - 1]) if q > 0 else jnp.zeros_like(here)
            xp = pltpu.roll(jnp.where(lane < nodes, following, here), LANES - nodes, 1)
            xm = pltpu.roll(jnp.where(lane >= LANES - nodes, previous, here), nodes, 1)
            return (xp + xm) + (pltpu.roll(here, size - 1, 0) + pltpu.roll(here, 1, 0))

        def finish(value, view):
            return 0.5 * value if step == 0 else value - load(view)

        for q in range(quads):
            flow = load(coef_ref.at[1, q]) * (load(pot_ref.at[now, q]) - load(col_ref.at[now, q]))
            store(flow_ref.at[q], flow)
            top = flow.astype(jnp.bfloat16)
            rest = flow - top.astype(jnp.float32)
            middle = rest.astype(jnp.bfloat16)
            rest = rest - middle.astype(jnp.float32)
            pieces = jnp.concatenate([top, middle, rest.astype(jnp.bfloat16)], axis=0)
            means = jnp.dot(pieces, mean_mat, preferred_element_type=jnp.float32)
            store(mean_ref.at[q], means[:size] + (means[size : 2 * size] + means[2 * size :]))
        wanted = SHELLS - step
        last = (lane % nodes) == (nodes - 1)
        for q in range(quads):
            flow = load(flow_ref.at[q])
            inside = load(coef_ref.at[1, q]) > 0.0
            diff = load(coef_ref.at[0, q])
            shell = load(shell_ref.at[now, 0, q])
            surface = shell
            fall_before = None
            for k in range(wanted):
                deeper = load(shell_ref.at[now, k + 1, q])
                fall = shell - deeper
                if k == 0:
                    value = KEEP * shell + (diff * fall + GAIN * flow)
                else:
                    value = KEEP * shell + diff * (fall - fall_before)
                view = shell_ref.at[old, k, q]
                store(view, finish(value, view))
                shell, fall_before = deeper, fall
            pots = load(pot_ref.at[now, q])
            drop = jnp.where(last, 0.0, pots - pltpu.roll(pots, LANES - 1, 1))
            value = (
                node_cond * (drop - pltpu.roll(drop, 1, 1))
                + (flow - load(coef_ref.at[2, q]) * surface)
                + (4.0 * plane_cond - CENTER) * pots
                - plane_cond * around(pot_ref, q)
            )
            view = pot_ref.at[old, q]
            store(view, jnp.where(inside, finish(GAIN * value, view), 0.0))
            coll = load(col_ref.at[now, q])
            value = (
                (4.0 * collector_cond - CENTER) * coll
                - collector_cond * around(col_ref, q)
                - load(mean_ref.at[q])
            )
            view = col_ref.at[old, q]
            store(view, jnp.where(inside, finish(GAIN * value, view), 0.0))
        own_ref[step * ys : (step + 1) * ys, :] = own_of(flow_ref[quad, 0:ys, :])

    own_ref[ITERS * ys :, :] = jnp.zeros((own_ref.shape[0] - ITERS * ys, LANES), jnp.float32)
    turned = [own_ref[at : at + LANES, :].T for at in range(0, own_ref.shape[0], LANES)]
    flows = [
        GAIN * turn_nodes(turned[step * ys // LANES], step * ys % LANES, rows, ys, nodes)
        for step in range(ITERS)
    ]
    sub = lax.broadcasted_iota(jnp.int32, (24, LANES), 0)
    for row in range(8):
        gain = jnp.broadcast_to(coeft_ref[0, row : row + 1, :], (24, LANES))
        keep = jnp.broadcast_to(coeft_ref[1, row : row + 1, :], (24, LANES))
        now, old = basis_ref[0, row, NR - 24 :, :], None
        outer_ref[0, row] = now[8:]
        for step in range(ITERS):
            prev = jnp.where(sub == 0, now, pltpu.roll(now, 1, 0))
            following = jnp.where(sub == 23, now, pltpu.roll(now, 23, 0))
            flow = jnp.broadcast_to(flows[step][row : row + 1, :], (24, LANES))
            value = keep * now - gain * (prev + following) + jnp.where(sub == 23, flow, 0.0)
            value = 0.5 * value if step == 0 else value - old
            now, old = value, now
            room_for(step + 1)[row] = now[8:]

    acc_ref[...] = jnp.zeros(acc_ref.shape, jnp.float32)
    inside = jnp.where(lax.broadcasted_iota(jnp.int32, (16, LANES), 0) >= 16 - ITERS, 1.0, 0.0)

    def gram_row(at, carry):
        mask = jnp.where(at < 8, inside, 1.0)
        add_gram([outer_ref[k, at] for k in range(ITERS)] + [tail_ref[at]], mask, acc_ref)
        return carry

    lax.fori_loop(0, 9, gram_row, 0)
    total = lane_totals(acc_ref, gram_ref.shape[0])
    gram_ref[...] = total + jnp.broadcast_to(inner_ref[0:1, :], total.shape)


def solve_kernel(
    sums_ref, basis_ref, outer_ref, conc_out, pots_out, flag_ref, conc_ref, pots_ref, sems
):
    rows, ys, width = conc_ref.shape
    nodes = pots_ref.shape[2] - 1
    half = rows * nodes
    side = 16
    total = jnp.sum(sums_ref[...], axis=0, keepdims=True)
    shape = (side, LANES)
    row = lax.broadcasted_iota(jnp.int32, shape, 0)
    col = lanes_of(shape)
    small = jnp.minimum(row, col)
    large = jnp.maximum(row, col)
    index = small * KV - (small * (small - 1)) // 2 + (large - small)
    valid = (row < KV) & (col < KV)
    index = jnp.where(valid, index, 0)
    gram = jnp.where(valid, pick(jnp.broadcast_to(total, shape), index), 0.0)
    eye = (row == col).astype(jnp.float32)

    def lane_sum(value):
        return jnp.sum(value, axis=1, keepdims=True)

    def sub_sum(value):
        return jnp.sum(value, axis=0, keepdims=True)

    column = (side, 1)
    crow = lax.broadcasted_iota(jnp.int32, column, 0)
    norm0 = gram[0:1, 0:1]
    beta = jnp.sqrt(norm0 + epsilon)
    coeffs = []
    images = []
    q = jnp.where(crow == 0, 1.0, 0.0) / beta
    gq = lane_sum(jnp.where(col == 0, gram, 0.0)) / beta
    table = jnp.where(col == 0, q, 0.0)
    gtable = jnp.where(col == 0, gq, 0.0)
    diag = lane_sum(gram * eye)
    columns = []
    coeffs.append(q)
    worst = jnp.zeros((1, 1), jnp.float32)
    for step in range(ITERS):
        down = pltpu.roll(jnp.broadcast_to(q, shape), 1, 0)
        up = jnp.where(
            row < side - 1, pltpu.roll(jnp.broadcast_to(q, shape), side - 1, 0), 0.0
        )
        q_full = jnp.broadcast_to(q, shape)
        first = jnp.broadcast_to(q[0:1], shape)
        w = CENTER * q_full + (0.5 * HALF) * (down + up) + jnp.where(
            row == 1, (0.5 * HALF) * first, 0.0
        )
        w_row = sub_sum(eye * w)
        g = lane_sum(gram * w_row)
        h_row = sub_sum(table * g)
        u = w[:, 0:1] - lane_sum(table * h_row)
        gu = g - lane_sum(gtable * h_row)
        square = sub_sum(u * gu)
        height = jnp.sqrt(square + epsilon)
        inverse = 1.0 / height
        q = u * inverse
        gq = gu * inverse
        columns.append(
            [lane_sum(jnp.where(lanes_of((1, LANES)) == i, h_row, 0.0)) for i in range(step + 1)]
            + [height]
        )
        coeffs.append(q)
        if step < ITERS - 1:
            table = jnp.where(col == step + 1, q, table)
            gtable = jnp.where(col == step + 1, gq, gtable)
        worst = jnp.maximum(worst, sub_sum(q * q * diag))
    good = (worst < INVERSE_MAX) & (norm0 > NORM_MIN)
    weights = least_squares(columns, beta)
    mix = weights[0] * coeffs[0]
    for step in range(1, ITERS):
        mix = mix + weights[step] * coeffs[step]
    bad = jnp.where(good & (jnp.abs(sub_sum(mix)) < 1e30), 0, 1)
    flag_ref[0] = jnp.max(bad)
    mix_full = jnp.broadcast_to(mix, shape)
    parts = [jnp.broadcast_to(mix_full[k : k + 1], (ys, LANES)) for k in range(ITERS)]

    def combine(ref, at):
        value = parts[0] * ref[(0, *at)]
        for k in range(1, ITERS):
            value = value + parts[k] * ref[(k, *at)]
        return value

    last = combine(outer_ref, (8,))
    for x in range(rows):
        pots_ref[x] = jnp.concatenate(
            [
                last[:, x * nodes : (x + 1) * nodes],
                last[:, half + x * nodes : half + x * nodes + 1],
            ],
            axis=1,
        )
    copies = [pltpu.make_async_copy(pots_ref, pots_out, sems.at[0])]
    copies[0].start()
    reached = lax.broadcasted_iota(jnp.int32, (16, LANES), 0) >= 16 - ITERS
    for group in range(4):
        pieces = []
        for at in (2 * group, 2 * group + 1):
            for base in range(0, NR - 16, 16):
                pieces.append(combine(basis_ref, (at, slice(base, base + 16))))
            pieces.append(
                jnp.where(
                    reached,
                    combine(outer_ref, (at,)),
                    combine(basis_ref, (at, slice(NR - 16, NR))),
                )
            )
        cells = jnp.concatenate(pieces, axis=0).T
        for slot in range(nodes // 8):
            tile = 4 * slot + group
            for x in range(rows):
                start = (slot * rows + x) * ys
                conc_ref[x, :, tile * LANES : (tile + 1) * LANES] = cells[start : start + ys]
    for x in range(rows):
        copy = pltpu.make_async_copy(conc_ref.at[x], conc_out.at[x], sems.at[1 + x])
        copy.start()
        copies.append(copy)
    for copy in copies:
        copy.wait()


def least_squares(columns, start_norm):
    count = len(columns)
    target = [start_norm] + [jnp.zeros_like(start_norm) for step in range(count)]
    cosines = []
    sines = []
    upper_rows = []
    for step in range(count):
        entries = list(columns[step])
        for row in range(step):
            first = cosines[row] * entries[row] + sines[row] * entries[row + 1]
            second = cosines[row] * entries[row + 1] - sines[row] * entries[row]
            entries[row] = first
            entries[row + 1] = second
        radius = jnp.sqrt(entries[step] * entries[step] + entries[step + 1] * entries[step + 1])
        cosine = entries[step] / radius
        sine = entries[step + 1] / radius
        entries[step] = radius
        cosines.append(cosine)
        sines.append(sine)
        lead = target[step]
        target[step] = cosine * lead
        target[step + 1] = -sine * lead
        upper_rows.append(entries[: step + 1])
    weights = [None] * count
    for row in range(count - 1, -1, -1):
        total = target[row]
        for later in range(row + 1, count):
            total = total - upper_rows[later][row] * weights[later]
        weights[row] = total / upper_rows[row][row]
    return weights


def shifted(cells, axis, dim):
    count = lax.axis_size(axis)
    size = cells.shape[dim]
    head = lax.slice_in_dim(cells, 0, 1, axis=dim)
    tail = lax.slice_in_dim(cells, size - 1, size, axis=dim)
    before = lax.ppermute(tail, axis, [(i, i + 1) for i in range(count - 1)])
    after = lax.ppermute(head, axis, [(i + 1, i) for i in range(count - 1)])
    padded = jnp.concatenate([before, cells, after], axis=dim)
    return lax.slice_in_dim(padded, 0, size, axis=dim), lax.slice_in_dim(padded, 2, size + 2, axis=dim)


def mirror_laplace(values):
    inner = jnp.concatenate([values[..., :1], values[..., :-1]], axis=-1)
    outer = jnp.concatenate([values[..., 1:], values[..., -1:]], axis=-1)
    return 2.0 * values - inner - outer


def local_operator(conc, pots, diffusion, exchange, slope):
    nodes = exchange.shape[2]
    shells = conc.reshape(conc.shape[0], conc.shape[1], nodes, NR)
    xm, xp = shifted(pots, "gx", 0)
    ym, yp = shifted(pots, "gy", 1)
    lateral = 4.0 * pots - xm - xp - ym - yp
    node_pot = pots[..., :nodes]
    current = exchange * (node_pot - pots[..., nodes:])
    flag = (lax.broadcasted_iota(jnp.int32, (NR,), 0) == NR - 1).astype(jnp.float32)
    new_shells = shells + diffusion[..., None] * mirror_laplace(shells) + current[..., None] * flag
    new_nodes = (
        node_cond * mirror_laplace(node_pot)
        + current
        - slope * shells[..., NR - 1]
        + plane_cond * lateral[..., :nodes]
    )
    new_collector = collector_cond * lateral[..., nodes:] - jnp.mean(current, axis=-1, keepdims=True)
    return new_shells.reshape(conc.shape), jnp.concatenate([new_nodes, new_collector], axis=-1)


def weights_kernel(hess_ref, out_ref):
    def entry(i, j):
        return hess_ref[j, i : i + 1, 0:1]

    columns = [[entry(i, j) for i in range(j + 2)] for j in range(ITERS)]
    start = hess_ref[ITERS, 0:1, 0:1]
    for k, weight in enumerate(least_squares(columns, start)):
        out_ref[k : k + 1, :] = jnp.broadcast_to(weight, (1, LANES))


def plain_cycle(rhs_conc, rhs_pots, diffusion, exchange, slope):
    axes = ("gx", "gy")
    square = jnp.sum(rhs_conc * rhs_conc) + jnp.sum(rhs_pots * rhs_pots)
    start = jnp.sqrt(lax.psum(square, axes) + epsilon)
    basis_c = jnp.zeros((KV,) + rhs_conc.shape, jnp.float32).at[0].set(rhs_conc / start)
    basis_p = jnp.zeros((KV,) + rhs_pots.shape, jnp.float32).at[0].set(rhs_pots / start)
    hess = jnp.zeros((KV, 16), jnp.float32).at[ITERS, 0].set(start)
    spot = jnp.arange(16)

    def body(step, carry):
        basis_c, basis_p, hess = carry
        conc = lax.dynamic_index_in_dim(basis_c, step, 0, False)
        pots = lax.dynamic_index_in_dim(basis_p, step, 0, False)
        image_c, image_p = local_operator(conc, pots, diffusion, exchange, slope)
        dots = jnp.sum(basis_c * image_c, axis=(1, 2, 3)) + jnp.sum(basis_p * image_p, axis=(1, 2, 3))
        dots = lax.psum(dots, axes)
        rest_c = image_c - jnp.sum(dots[:, None, None, None] * basis_c, axis=0)
        rest_p = image_p - jnp.sum(dots[:, None, None, None] * basis_p, axis=0)
        square = lax.psum(jnp.sum(rest_c * rest_c) + jnp.sum(rest_p * rest_p), axes)
        height = jnp.sqrt(square + epsilon)
        basis_c = lax.dynamic_update_index_in_dim(basis_c, rest_c / height, step + 1, 0)
        basis_p = lax.dynamic_update_index_in_dim(basis_p, rest_p / height, step + 1, 0)
        line = jnp.concatenate([dots, jnp.zeros((16 - KV,), jnp.float32)])
        line = jnp.where(spot == step + 1, height, line)
        hess = lax.dynamic_update_index_in_dim(hess, line, step, 0)
        return basis_c, basis_p, hess

    basis_c, basis_p, hess = lax.fori_loop(0, ITERS, body, (basis_c, basis_p, hess))
    wide = jnp.broadcast_to(hess[:, :, None], hess.shape + (LANES,))
    weights = pl.pallas_call(
        weights_kernel, out_shape=jax.ShapeDtypeStruct((16, LANES), jnp.float32)
    )(wide)[:KV, 0]
    weights = jnp.where(jnp.arange(KV) < ITERS, weights, 0.0)[:, None, None, None]
    return jnp.sum(weights * basis_c, axis=0), jnp.sum(weights * basis_p, axis=0)


def shards(rhs_conc, rhs_pots, diffusion, exchange, slope):
    rows, ys, nodes = exchange.shape
    gx, gy = lax.axis_size("gx"), lax.axis_size("gy")
    half = rows * nodes
    pairs = FIELDS // 2
    assert half * 2 == LANES and nodes * NR == rhs_conc.shape[2]
    assert ys == 16 and ITERS <= ys and gx % 2 == 0
    assert half * 2 == rows * nodes // 8 * ys and LANES == 2 * NR
    window = 8 * ((ys + 2 * ITERS + 1 + 7) // 8)
    f32 = jnp.float32
    vmem = pl.BlockSpec(memory_space=pltpu.VMEM)
    smem = pl.BlockSpec(memory_space=pltpu.SMEM)
    hbm = pl.BlockSpec(memory_space=pltpu.HBM)
    params = pltpu.CompilerParams(vmem_limit_bytes=24 << 20)

    send, up, down = pl.pallas_call(
        pack_kernel,
        out_shape=(
            jax.ShapeDtypeStruct((pairs * ys, LANES), f32),
            jax.ShapeDtypeStruct((EDGE, LANES), f32),
            jax.ShapeDtypeStruct((EDGE, LANES), f32),
        ),
        compiler_params=params,
    )(rhs_conc, rhs_pots, diffusion, exchange, slope)
    left = lax.ppermute(up, "gy", [(i, i + 1) for i in range(gy - 1)])
    right = lax.ppermute(down, "gy", [(i + 1, i) for i in range(gy - 1)])
    basis, coefs, deep, inner_gram = pl.pallas_call(
        free_kernel,
        out_shape=(
            jax.ShapeDtypeStruct((ITERS, 8, NR, LANES), f32),
            jax.ShapeDtypeStruct((2, 8, LANES), f32),
            jax.ShapeDtypeStruct((ys, LANES), f32),
            jax.ShapeDtypeStruct((8, LANES), f32),
        ),
        scratch_shapes=[
            pltpu.VMEM((8, NR, LANES), f32),
            pltpu.VMEM((LANES, 8, LANES), f32),
        ],
        compiler_params=params,
        cost_estimate=pl.CostEstimate(flops=20000000, transcendentals=0, bytes_accessed=3000000),
    )(rhs_conc, diffusion)
    left, right, inner_gram = lax.optimization_barrier((left, right, inner_gram))
    block = jnp.concatenate([send, left, right], axis=0)
    everything = lax.all_gather(block, "gx", axis=0, tiled=False)
    spot = lax.axis_index("gx").astype(jnp.int32).reshape(1)

    quads = gx // 2
    outer, gram = pl.pallas_call(
        functools.partial(powers_kernel, rows=rows, nodes=nodes),
        in_specs=[smem] + [vmem] * 5,
        out_specs=(vmem, vmem),
        out_shape=(
            jax.ShapeDtypeStruct((ITERS, 9, 16, LANES), f32),
            jax.ShapeDtypeStruct((gx * gy, LANES), f32),
        ),
        scratch_shapes=[
            pltpu.VMEM((2, quads, window, LANES), f32),
            pltpu.VMEM((2, quads, window, LANES), f32),
            pltpu.VMEM((2, SHELLS + 1, quads, window, LANES), f32),
            pltpu.VMEM((3, quads, window, LANES), f32),
            pltpu.VMEM((quads, window, LANES), f32),
            pltpu.VMEM((quads, window, LANES), f32),
            pltpu.VMEM((LANES * pl.cdiv(ITERS * ys, LANES), LANES), f32),
            pltpu.VMEM((9, 16, LANES), f32),
            pltpu.VMEM((LANES, 8, LANES), f32),
        ],
        compiler_params=params,
    )(spot, everything, basis, coefs, deep, inner_gram)

    sums = lax.all_to_all(gram, ("gx", "gy"), 0, 0, tiled=True)

    conc, pots, flag = pl.pallas_call(
        solve_kernel,
        out_shape=(
            jax.ShapeDtypeStruct(rhs_conc.shape, f32),
            jax.ShapeDtypeStruct(rhs_pots.shape, f32),
            jax.ShapeDtypeStruct((1,), jnp.int32),
        ),
        out_specs=(hbm, hbm, smem),
        scratch_shapes=[
            pltpu.VMEM(rhs_conc.shape, f32),
            pltpu.VMEM(rhs_pots.shape, f32),
            pltpu.SemaphoreType.DMA((rows + 1,)),
        ],
        compiler_params=params,
    )(sums, basis, outer)
    return lax.while_loop(
        lambda carry: carry[0] > 0,
        lambda carry: (0, *plain_cycle(rhs_conc, rhs_pots, diffusion, exchange, slope)),
        (flag[0], conc, pots),
    )[1:]


def solution(mesh):
    spec = P("gx", "gy", None)
    return jax.shard_map(
        shards, mesh=mesh, in_specs=(spec,) * 5, out_specs=(spec, spec), check_vma=False
    )
```

time: 52.9 us -> 45.9 us (0.87)
  blocking collectives: 10.5 us -> 23.5 us
  waiting for transfers between devices: 11.5 us -> 0.08 us
  starting transfers between devices: 10.1 us -> 6.25 us
  Pallas kernels: 17.5 us -> 14.2 us
  local copies, waits for them, and re-layouts: 1.31 us -> 0.01 us
  loops' own time: 0.23 us -> 0.79 us
  between operations: 1.38 us -> 0.83 us
    all_to_all x0 -> x1, blocking collectives: none -> 13 us  [shards(): sums = lax.all_to_all(gram, ('gx', 'gy'), 0, 0, tiled=True)]
    all_to_all x1 -> x0, waiting for transfers between devices: 7.12 us -> none  [shards(): sums = lax.all_to_all(gram, ('gx', 'gy'), 0, 0, tiled=True)]
    ppermute x1, waiting for transfers between devices: 4.22 us -> 0.07 us  [shards(): right = lax.ppermute(down, 'gy', [(i + 1, i) for i in range(gy - 1)])]
    all_to_all x1 -> x0, starting transfers between devices: 3.89 us -> none  [shards(): sums = lax.all_to_all(gram, ('gx', 'gy'), 0, 0, tiled=True)]
    pallas_call x1 -> x2, Pallas kernels: 11.3 us -> 8.36 us  [the longest x1 4.34 us: shards(): pl.pallas_call(free_kernel, out_shape=(jax.ShapeDtypeStruct((ITERS, 8, NR...]
    unnamed x8 -> x2, local copies, waits for them, and re-layouts: 1.31 us -> 0.01 us
    pallas_call x1, Pallas kernels: 2.69 us -> 1.43 us  [shards(): pl.pallas_call(pack_kernel, out_shape=(jax.ShapeDtypeStruct((pairs * ys,...]
    pallas_call x1, Pallas kernels: 3.46 us -> 4.44 us  [shards(): pl.pallas_call(solve_kernel, out_shape=(jax.ShapeDtypeStruct(rhs_conc.sha...]
  transfers between devices with their start and end apart: 3 -> 2, of which waited for: 3 -> 1; matrix products, arithmetic and copies ran while one was open for 0% -> 0% of each run, Pallas kernels for 0% -> 9%
where the time goes in v3:
time: 45.9 us; the launch traced here: 45.7 us
  blocking collectives  23.5 us (51%)
  Pallas kernels  14.2 us (31%)
  starting transfers between devices  6.25 us (14%)
  between operations  0.83 us (2%)
  loops' own time  0.79 us (2%)
    all_to_all x1, blocking collectives, shards(): sums = lax.all_to_all(gram, ('gx', 'gy'), 0, 0, tiled=True)  13 us
    all_gather x1, blocking collectives, shards(): everything = lax.all_gather(block, 'gx', axis=0, tiled=False)  10.5 us
    ppermute x1, starting transfers between devices, shards(): left = lax.ppermute(up, 'gy', [(i, i + 1) for i in range(gy - 1)])  4.96 us
    pallas_call x1, Pallas kernels, shards(): pl.pallas_call(solve_kernel, out_shape=(jax.ShapeDtypeStruct(rhs_conc.sha...  4.44 us
    pallas_call x1, Pallas kernels, shards(): pl.pallas_call(free_kernel, out_shape=(jax.ShapeDtypeStruct((ITERS, 8, NR...  4.34 us
    pallas_call x1, Pallas kernels, shards(): pl.pallas_call(functools.partial(powers_kernel, rows=rows, nodes=nodes),...  4.02 us
    pallas_call x1, Pallas kernels, shards(): pl.pallas_call(pack_kernel, out_shape=(jax.ShapeDtypeStruct((pairs * ys,...  1.43 us
    ppermute x1, starting transfers between devices, shards(): right = lax.ppermute(down, 'gy', [(i + 1, i) for i in range(gy - 1)])  1.29 us
  transfers between devices with their start and end apart: 2, of which 1 were waited for; matrix products, arithmetic and copies ran while one was open for 0% of the time, Pallas kernels for 9%

profile of v3, /device:TPU:0, one launch (start us, length us, event | category | flops | bytes accessed | tf_op | source)
XLA Modules:
  0.0 45.7 jit_solution(5007213270784096365)
XLA Ops:
  0.6 1.4 %shard_map.68 = (f32[112,128]{1,0:T(8,128)S(1)}, f32[48,128]{1,0:T(8,128)S(1)}, f32[48,128]{1,0:T(8,128)S(1)}) custom-call(f32[2,16,2048]{2,1,0:T(8,128)} %conc_ref.3, f32[2,16,33]{2,1,0:T(8,128)} %pots_ref.1, f32[2,16,32]{2,1,0:T(8,128)} %diff_ref.3, f32[2,16,32]{2,1,0:T(8,128)} %exch_ref.1, f32[2,16,32]{2,1,0:T(8,128)} %slope_ref.1), custom_call_target="tpu_custom_call" | custom-call | tf_op jit(solution)/shard_map/pallas_call | solution.py:614
  2.1 5.0 %collective-permute-start.4 = (f32[48,128]{1,0:T(8,128)S(1)}, f32[48,128]{1,0:T(8,128)S(1)}, u32[]{:S(2)}, u32[]{:S(2)}) collective-permute-start(f32[48,128]{1,0:T(8,128)S(1)} %get-tuple-element.294), channel_id=1, source_target_pairs={{0,1},{1,2},{2,3},{4,5},{5,6},{6,7},{8,9},{9,10},{10,11},{12,13},{... | collective-permute-start | bytes 73736 | tf_op jit(solution)/shard_map/ppermute | solution.py:623
  7.0 1.3 %collective-permute-start.5 = (f32[48,128]{1,0:T(8,128)S(1)}, f32[48,128]{1,0:T(8,128)S(1)}, u32[]{:S(2)}, u32[]{:S(2)}) collective-permute-start(f32[48,128]{1,0:T(8,128)S(1)} %get-tuple-element.295), channel_id=1, source_target_pairs={{1,0},{2,1},{3,2},{5,4},{6,5},{7,6},{9,8},{10,9},{11,10},{13,12},{... | collective-permute-start | bytes 73736 | tf_op jit(solution)/shard_map/ppermute | solution.py:624
  8.3 4.3 %shard_map.69 = (f32[10,8,64,128]{3,2,1,0:T(8,128)S(1)}, f32[2,8,128]{2,1,0:T(8,128)S(1)}, f32[16,128]{1,0:T(8,128)S(1)}, f32[8,128]{1,0:T(8,128)S(1)}) custom-call(f32[2,16,2048]{2,1,0:T(8,128)} %conc_ref.3, f32[2,16,32]{2,1,0:T(8,128)} %diff_ref.3), custom_call_target="tpu_custom_call" | custom-call | flops 20000000 | bytes 3000000 | tf_op jit(solution)/shard_map/pallas_call | solution.py:625
  12.7 0.0 collective-permute-done.4
  12.7 0.1 collective-permute-done.5
  12.8 10.5 %all-gather = f32[1664,128]{1,0:T(8,128)S(1)} all-gather(f32[208,128]{1,0:T(8,128)S(1)} %pad_maximum_fusion.7), channel_id=2, replica_groups=mesh['gx'=8,'gy'=4] {'gx'}, dimensions={0}, use_global_device_ids=true | all-gather | bytes 958464 | tf_op jit(solution)/shard_map/all_gather | solution.py:642
  23.3 0.0 copy-start.6
  23.3 4.0 %shard_map.70 = (f32[10,9,16,128]{3,2,1,0:T(8,128)S(1)}, f32[32,128]{1,0:T(8,128)S(1)}) custom-call(s32[1]{0:T(128)} %bitcast.3.spot_ref, f32[8,208,128]{2,1,0:T(8,128)S(1)} %bitcast.90, f32[10,8,64,128]{3,2,1,0:T(8,128)S(1)} %get-tuple-element.299.basis_ref, f32[2,8,128]{2,1,0:T(8,128)S(1)} %get-tuple-element.300.coeft_ref, ...), custom_call_target="tpu_custom_call" | custom-call | tf_op jit(solution)/shard_map/pallas_call | solution.py:646
  27.3 13.0 %all_to_all.11 = f32[32,1,128]{2,1,0:T(1,128)S(1)} all-to-all(f32[32,1,128]{2,1,0:T(1,128)S(1)} %bitcast.92), channel_id=1, replica_groups=mesh['gx'=8,'gy'=4] {'gx','gy'}, dimensions={0} | all-to-all | bytes 32768 | tf_op jit(solution)/shard_map/all_to_all | solution.py:668
  40.3 4.4 %shard_map.71 = (f32[2,16,2048]{2,1,0:T(8,128)}, f32[2,16,33]{2,1,0:T(8,128)}, s32[1]{0:T(128)}) custom-call(f32[32,128]{1,0:T(8,128)S(1)} %bitcast.91, f32[10,8,64,128]{3,2,1,0:T(8,128)S(1)} %get-tuple-element.299.basis_ref, f32[10,9,16,128]{3,2,1,0:T(8,128)S(1)} %get-tuple-element.304.outer_ref), custom_call_target="tpu_custom_call" | custom-call | tf_op jit(solution)/shard_map/pallas_call | solution.py:670
  44.7 0.0 copy-done.6
  44.7 0.8 %while.32 = (s32[]{:T(128)}, f32[2,16,2048]{2,1,0:T(8,128)}, f32[2,16,33]{2,1,0:T(8,128)}, f32[2,16,2048]{2,1,0:T(8,128)S(1)}, f32[2,16,33]{2,1,0:T(8,128)}, /*i...) while((s32[]{:T(128)}, f32[2,16,2048]{2,1,0:T(8,128)}, ...), condition=%region_17.18_spmd, body=%region_0.17_spmd | while | flops 5869439 | bytes 33019008 | solution.py:685
  (1 shorter events, 0.0 us)
Async XLA Ops:
  2.1 10.6 %collective-permute-start.4 = (f32[48,128]{1,0:T(8,128)S(1)}, f32[48,128]{1,0:T(8,128)S(1)}, u32[]{:S(2)}, u32[]{:S(2)}) collective-permute-start(f32[48,128]{1,0:T(8,128)S(1)} %get-tuple-element.294), channel_id=1, source_target_pairs={{0,1},{1,2},{2,3},{4,5},{5,6},{6,7},{8,9},{9,10},{10,11},{12,13},{... | collective-permute-start | bytes 73736 | tf_op jit(solution)/shard_map/ppermute | solution.py:623
  7.0 5.7 %collective-permute-start.5 = (f32[48,128]{1,0:T(8,128)S(1)}, f32[48,128]{1,0:T(8,128)S(1)}, u32[]{:S(2)}, u32[]{:S(2)}) collective-permute-start(f32[48,128]{1,0:T(8,128)S(1)} %get-tuple-element.295), channel_id=1, source_target_pairs={{1,0},{2,1},{3,2},{5,4},{6,5},{7,6},{9,8},{10,9},{11,10},{13,12},{... | collective-permute-start | bytes 73736 | tf_op jit(solution)/shard_map/ppermute | solution.py:624
  23.3 21.4 %copy-start.6 = (f32[2,16,2048]{2,1,0:T(8,128)S(1)}, f32[2,16,2048]{2,1,0:T(8,128)}, u32[]{:S(2)}) copy-start(f32[2,16,2048]{2,1,0:T(8,128)} %conc_ref.3) | copy-start | bytes 786436

commit v4 on v3

--- a/solution.py
+++ b/solution.py
@@ -376,66 +376,53 @@
     valid = (row < KV) & (col < KV)
     index = jnp.where(valid, index, 0)
     gram = jnp.where(valid, pick(jnp.broadcast_to(total, shape), index), 0.0)
-    eye = (row == col).astype(jnp.float32)
-
-    def lane_sum(value):
-        return jnp.sum(value, axis=1, keepdims=True)
 
     def sub_sum(value):
         return jnp.sum(value, axis=0, keepdims=True)
 
-    column = (side, 1)
-    crow = lax.broadcasted_iota(jnp.int32, column, 0)
+    def full(value):
+        return jnp.broadcast_to(value, shape)
+
+    grams = [full(gram[:, k : k + 1]) for k in range(KV)]
+    diag = jnp.zeros(shape, jnp.float32)
+    for k in range(KV):
+        diag = jnp.where(row == k, grams[k], diag)
+    shifted_grams = [CENTER * grams[0] + HALF * grams[1]]
+    for k in range(1, ITERS):
+        shifted_grams.append(CENTER * grams[k] + (0.5 * HALF) * (grams[k - 1] + grams[k + 1]))
     norm0 = gram[0:1, 0:1]
-    beta = jnp.sqrt(norm0 + epsilon)
-    coeffs = []
-    images = []
-    q = jnp.where(crow == 0, 1.0, 0.0) / beta
-    gq = lane_sum(jnp.where(col == 0, gram, 0.0)) / beta
-    table = jnp.where(col == 0, q, 0.0)
-    gtable = jnp.where(col == 0, gq, 0.0)
-    diag = lane_sum(gram * eye)
+    start = full(norm0) + epsilon
+    inverse = lax.rsqrt(start)
+    beta = (start * inverse)[0:1]
+    coeffs = [jnp.where(row == 0, inverse, 0.0)]
+    images = [grams[0] * inverse]
     columns = []
-    coeffs.append(q)
-    worst = jnp.zeros((1, 1), jnp.float32)
+    worst = jnp.zeros((1, LANES), jnp.float32)
     for step in range(ITERS):
-        down = pltpu.roll(jnp.broadcast_to(q, shape), 1, 0)
-        up = jnp.where(
-            row < side - 1, pltpu.roll(jnp.broadcast_to(q, shape), side - 1, 0), 0.0
-        )
-        q_full = jnp.broadcast_to(q, shape)
-        first = jnp.broadcast_to(q[0:1], shape)
-        w = CENTER * q_full + (0.5 * HALF) * (down + up) + jnp.where(
-            row == 1, (0.5 * HALF) * first, 0.0
-        )
-        w_row = sub_sum(eye * w)
-        g = lane_sum(gram * w_row)
-        h_row = sub_sum(table * g)
-        u = w[:, 0:1] - lane_sum(table * h_row)
-        gu = g - lane_sum(gtable * h_row)
-        square = sub_sum(u * gu)
-        height = jnp.sqrt(square + epsilon)
-        inverse = 1.0 / height
-        q = u * inverse
-        gq = gu * inverse
-        columns.append(
-            [lane_sum(jnp.where(lanes_of((1, LANES)) == i, h_row, 0.0)) for i in range(step + 1)]
-            + [height]
-        )
-        coeffs.append(q)
-        if step < ITERS - 1:
-            table = jnp.where(col == step + 1, q, table)
-            gtable = jnp.where(col == step + 1, gq, gtable)
-        worst = jnp.maximum(worst, sub_sum(q * q * diag))
+        q = coeffs[step]
+        entries = [full(q[k : k + 1]) for k in range(step + 1)]
+        down = pltpu.roll(q, 1, 0)
+        up = jnp.where(row < side - 1, pltpu.roll(q, side - 1, 0), 0.0)
+        w = CENTER * q + (0.5 * HALF) * (down + up)
+        w = w + jnp.where(row == 1, (0.5 * HALF) * entries[0], 0.0)
+        g = tree_sum([shifted_grams[k] * entries[k] for k in range(step + 1)])
+        heads = [sub_sum(coeffs[i] * g) for i in range(step + 1)]
+        wide = [full(value) for value in heads]
+        u = w - tree_sum([wide[i] * coeffs[i] for i in range(step + 1)])
+        gu = g - tree_sum([wide[i] * images[i] for i in range(step + 1)])
+        square = sub_sum(u * gu) + epsilon
+        inverse = lax.rsqrt(square)
+        columns.append(heads + [square * inverse])
+        inverse = full(inverse)
+        coeffs.append(u * inverse)
+        images.append(gu * inverse)
+        worst = jnp.maximum(worst, sub_sum(coeffs[-1] * coeffs[-1] * diag))
     good = (worst < INVERSE_MAX) & (norm0 > NORM_MIN)
     weights = least_squares(columns, beta)
-    mix = weights[0] * coeffs[0]
-    for step in range(1, ITERS):
-        mix = mix + weights[step] * coeffs[step]
+    mix = tree_sum([full(weights[step]) * coeffs[step] for step in range(ITERS)])
     bad = jnp.where(good & (jnp.abs(sub_sum(mix)) < 1e30), 0, 1)
     flag_ref[0] = jnp.max(bad)
-    mix_full = jnp.broadcast_to(mix, shape)
-    parts = [jnp.broadcast_to(mix_full[k : k + 1], (ys, LANES)) for k in range(ITERS)]
+    parts = [jnp.broadcast_to(mix[k : k + 1], (ys, LANES)) for k in range(ITERS)]
 
     def combine(ref, at):
         value = parts[0] * ref[(0, *at)]
@@ -473,12 +460,21 @@
             for x in range(rows):
                 start = (slot * rows + x) * ys
                 conc_ref[x, :, tile * LANES : (tile + 1) * LANES] = cells[start : start + ys]
-    for x in range(rows):
-        copy = pltpu.make_async_copy(conc_ref.at[x], conc_out.at[x], sems.at[1 + x])
-        copy.start()
-        copies.append(copy)
+            view = (slice(None), slice(None), slice(tile * LANES, (tile + 1) * LANES))
+            copy = pltpu.make_async_copy(conc_ref.at[view], conc_out.at[view], sems.at[1 + tile])
+            copy.start()
+            copies.append(copy)
     for copy in copies:
         copy.wait()
+
+
+def tree_sum(values):
+    while len(values) > 1:
+        values = [
+            values[i] + values[i + 1] if i + 1 < len(values) else values[i]
+            for i in range(0, len(values), 2)
+        ]
+    return values[0]
 
 
 def least_squares(columns, start_norm):
@@ -487,6 +483,7 @@
     cosines = []
     sines = []
     upper_rows = []
+    inverses = []
     for step in range(count):
         entries = list(columns[step])
         for row in range(step):
@@ -494,22 +491,22 @@
             second = cosines[row] * entries[row + 1] - sines[row] * entries[row]
             entries[row] = first
             entries[row + 1] = second
-        radius = jnp.sqrt(entries[step] * entries[step] + entries[step + 1] * entries[step + 1])
-        cosine = entries[step] / radius
-        sine = entries[step + 1] / radius
-        entries[step] = radius
+        inverse = lax.rsqrt(entries[step] * entries[step] + entries[step + 1] * entries[step + 1])
+        cosine = entries[step] * inverse
+        sine = entries[step + 1] * inverse
+        inverses.append(inverse)
         cosines.append(cosine)
         sines.append(sine)
         lead = target[step]
         target[step] = cosine * lead
         target[step + 1] = -sine * lead
-        upper_rows.append(entries[: step + 1])
+        upper_rows.append(entries[:step])
     weights = [None] * count
     for row in range(count - 1, -1, -1):
         total = target[row]
-        for later in range(row + 1, count):
+        for later in range(count - 1, row, -1):
             total = total - upper_rows[later][row] * weights[later]
-        weights[row] = total / upper_rows[row][row]
+        weights[row] = total * inverses[row]
     return weights
 
 
@@ -678,7 +675,7 @@
         scratch_shapes=[
             pltpu.VMEM(rhs_conc.shape, f32),
             pltpu.VMEM(rhs_pots.shape, f32),
-            pltpu.SemaphoreType.DMA((rows + 1,)),
+            pltpu.SemaphoreType.DMA((1 + nodes * NR // LANES,)),
         ],
         compiler_params=params,
     )(sums, basis, outer)

time: 45.9 us -> 43.7 us (0.952)
  Pallas kernels: 14.2 us -> 12 us
    pallas_call x1, Pallas kernels: 4.44 us -> 2.18 us  [shards(): pl.pallas_call(solve_kernel, out_shape=(jax.ShapeDtypeStruct(rhs_conc.sha...]
  transfers between devices with their start and end apart: 2 -> 2, of which waited for: 1 -> 1; matrix products, arithmetic and copies ran while one was open for 0% -> 0% of each run, Pallas kernels for 9% -> 10%
where the time goes in v4:
time: 43.7 us; the launch traced here: 43.4 us
  blocking collectives  23.5 us (54%)
  Pallas kernels  12 us (27%)
  starting transfers between devices  6.25 us (14%)
  between operations  0.83 us (2%)
  loops' own time  0.79 us (2%)
    all_to_all x1, blocking collectives, shards(): sums = lax.all_to_all(gram, ('gx', 'gy'), 0, 0, tiled=True)  13 us
    all_gather x1, blocking collectives, shards(): everything = lax.all_gather(block, 'gx', axis=0, tiled=False)  10.5 us
    ppermute x1, starting transfers between devices, shards(): left = lax.ppermute(up, 'gy', [(i, i + 1) for i in range(gy - 1)])  4.96 us
    pallas_call x1, Pallas kernels, shards(): pl.pallas_call(free_kernel, out_shape=(jax.ShapeDtypeStruct((ITERS, 8, NR...  4.34 us
    pallas_call x1, Pallas kernels, shards(): pl.pallas_call(functools.partial(powers_kernel, rows=rows, nodes=nodes),...  4.02 us
    pallas_call x1, Pallas kernels, shards(): pl.pallas_call(solve_kernel, out_shape=(jax.ShapeDtypeStruct(rhs_conc.sha...  2.18 us
    pallas_call x1, Pallas kernels, shards(): pl.pallas_call(pack_kernel, out_shape=(jax.ShapeDtypeStruct((pairs * ys,...  1.43 us
    ppermute x1, starting transfers between devices, shards(): right = lax.ppermute(down, 'gy', [(i + 1, i) for i in range(gy - 1)])  1.29 us
  transfers between devices with their start and end apart: 2, of which 1 were waited for; matrix products, arithmetic and copies ran while one was open for 0% of the time, Pallas kernels for 10%

profile of v4, /device:TPU:0, one launch (start us, length us, event | category | flops | bytes accessed | tf_op | source)
XLA Modules:
  0.0 43.4 jit_solution(17137528139104321431)
XLA Ops:
  0.6 1.4 %shard_map.68 = (f32[112,128]{1,0:T(8,128)S(1)}, f32[48,128]{1,0:T(8,128)S(1)}, f32[48,128]{1,0:T(8,128)S(1)}) custom-call(f32[2,16,2048]{2,1,0:T(8,128)} %conc_ref.3, f32[2,16,33]{2,1,0:T(8,128)} %pots_ref.1, f32[2,16,32]{2,1,0:T(8,128)} %diff_ref.3, f32[2,16,32]{2,1,0:T(8,128)} %exch_ref.1, f32[2,16,32]{2,1,0:T(8,128)} %slope_ref.1), custom_call_target="tpu_custom_call" | custom-call | tf_op jit(solution)/shard_map/pallas_call | solution.py:611
  2.1 5.0 %collective-permute-start.4 = (f32[48,128]{1,0:T(8,128)S(1)}, f32[48,128]{1,0:T(8,128)S(1)}, u32[]{:S(2)}, u32[]{:S(2)}) collective-permute-start(f32[48,128]{1,0:T(8,128)S(1)} %get-tuple-element.294), channel_id=1, source_target_pairs={{0,1},{1,2},{2,3},{4,5},{5,6},{6,7},{8,9},{9,10},{10,11},{12,13},{... | collective-permute-start | bytes 73736 | tf_op jit(solution)/shard_map/ppermute | solution.py:620
  7.0 1.3 %collective-permute-start.5 = (f32[48,128]{1,0:T(8,128)S(1)}, f32[48,128]{1,0:T(8,128)S(1)}, u32[]{:S(2)}, u32[]{:S(2)}) collective-permute-start(f32[48,128]{1,0:T(8,128)S(1)} %get-tuple-element.295), channel_id=1, source_target_pairs={{1,0},{2,1},{3,2},{5,4},{6,5},{7,6},{9,8},{10,9},{11,10},{13,12},{... | collective-permute-start | bytes 73736 | tf_op jit(solution)/shard_map/ppermute | solution.py:621
  8.3 4.3 %shard_map.69 = (f32[10,8,64,128]{3,2,1,0:T(8,128)S(1)}, f32[2,8,128]{2,1,0:T(8,128)S(1)}, f32[16,128]{1,0:T(8,128)S(1)}, f32[8,128]{1,0:T(8,128)S(1)}) custom-call(f32[2,16,2048]{2,1,0:T(8,128)} %conc_ref.3, f32[2,16,32]{2,1,0:T(8,128)} %diff_ref.3), custom_call_target="tpu_custom_call" | custom-call | flops 20000000 | bytes 3000000 | tf_op jit(solution)/shard_map/pallas_call | solution.py:622
  12.7 0.0 collective-permute-done.4
  12.7 0.1 collective-permute-done.5
  12.8 10.5 %all-gather = f32[1664,128]{1,0:T(8,128)S(1)} all-gather(f32[208,128]{1,0:T(8,128)S(1)} %pad_maximum_fusion.7), channel_id=2, replica_groups=mesh['gx'=8,'gy'=4] {'gx'}, dimensions={0}, use_global_device_ids=true | all-gather | bytes 958464 | tf_op jit(solution)/shard_map/all_gather | solution.py:639
  23.3 0.0 copy-start.6
  23.3 4.0 %shard_map.70 = (f32[10,9,16,128]{3,2,1,0:T(8,128)S(1)}, f32[32,128]{1,0:T(8,128)S(1)}) custom-call(s32[1]{0:T(128)} %bitcast.3.spot_ref, f32[8,208,128]{2,1,0:T(8,128)S(1)} %bitcast.90, f32[10,8,64,128]{3,2,1,0:T(8,128)S(1)} %get-tuple-element.299.basis_ref, f32[2,8,128]{2,1,0:T(8,128)S(1)} %get-tuple-element.300.coeft_ref, ...), custom_call_target="tpu_custom_call" | custom-call | tf_op jit(solution)/shard_map/pallas_call | solution.py:643
  27.3 13.0 %all_to_all.11 = f32[32,1,128]{2,1,0:T(1,128)S(1)} all-to-all(f32[32,1,128]{2,1,0:T(1,128)S(1)} %bitcast.92), channel_id=1, replica_groups=mesh['gx'=8,'gy'=4] {'gx','gy'}, dimensions={0} | all-to-all | bytes 32768 | tf_op jit(solution)/shard_map/all_to_all | solution.py:665
  40.3 2.2 %shard_map.71 = (f32[2,16,2048]{2,1,0:T(8,128)}, f32[2,16,33]{2,1,0:T(8,128)}, s32[1]{0:T(128)}) custom-call(f32[32,128]{1,0:T(8,128)S(1)} %bitcast.91, f32[10,8,64,128]{3,2,1,0:T(8,128)S(1)} %get-tuple-element.299.basis_ref, f32[10,9,16,128]{3,2,1,0:T(8,128)S(1)} %get-tuple-element.304.outer_ref), custom_call_target="tpu_custom_call" | custom-call | tf_op jit(solution)/shard_map/pallas_call | solution.py:667
  42.5 0.0 copy-done.6
  42.5 0.8 %while.32 = (s32[]{:T(128)}, f32[2,16,2048]{2,1,0:T(8,128)}, f32[2,16,33]{2,1,0:T(8,128)}, f32[2,16,2048]{2,1,0:T(8,128)S(1)}, f32[2,16,33]{2,1,0:T(8,128)}, /*i...) while((s32[]{:T(128)}, f32[2,16,2048]{2,1,0:T(8,128)}, ...), condition=%region_17.18_spmd, body=%region_0.17_spmd | while | flops 5869439 | bytes 33019008 | solution.py:682
  (1 shorter events, 0.0 us)
Async XLA Ops:
  2.1 10.6 %collective-permute-start.4 = (f32[48,128]{1,0:T(8,128)S(1)}, f32[48,128]{1,0:T(8,128)S(1)}, u32[]{:S(2)}, u32[]{:S(2)}) collective-permute-start(f32[48,128]{1,0:T(8,128)S(1)} %get-tuple-element.294), channel_id=1, source_target_pairs={{0,1},{1,2},{2,3},{4,5},{5,6},{6,7},{8,9},{9,10},{10,11},{12,13},{... | collective-permute-start | bytes 73736 | tf_op jit(solution)/shard_map/ppermute | solution.py:620
  7.0 5.7 %collective-permute-start.5 = (f32[48,128]{1,0:T(8,128)S(1)}, f32[48,128]{1,0:T(8,128)S(1)}, u32[]{:S(2)}, u32[]{:S(2)}) collective-permute-start(f32[48,128]{1,0:T(8,128)S(1)} %get-tuple-element.295), channel_id=1, source_target_pairs={{1,0},{2,1},{3,2},{5,4},{6,5},{7,6},{9,8},{10,9},{11,10},{13,12},{... | collective-permute-start | bytes 73736 | tf_op jit(solution)/shard_map/ppermute | solution.py:621
  23.3 19.2 %copy-start.6 = (f32[2,16,2048]{2,1,0:T(8,128)S(1)}, f32[2,16,2048]{2,1,0:T(8,128)}, u32[]{:S(2)}) copy-start(f32[2,16,2048]{2,1,0:T(8,128)} %conc_ref.3) | copy-start | bytes 786436

commit v5 on v4

--- a/solution.py
+++ b/solution.py
@@ -38,11 +38,16 @@
     return jnp.take_along_axis(values, index, axis=1, mode="promise_in_bounds")
 
 
-def pack_kernel(conc_ref, pots_ref, diff_ref, exch_ref, slope_ref, send_ref, up_ref, down_ref):
+def pack_kernel(
+    conc_ref, pots_ref, diff_ref, exch_ref, slope_ref, send_ref, up_ref, down_ref, copy_ref, spread_ref
+):
     rows, ys, nodes = exch_ref.shape
     half = rows * nodes
     lane = lanes_of((ys, LANES))
     low = lane < half
+    copy_ref[...] = conc_ref[...]
+    for x in range(rows):
+        spread_ref[x] = diff_ref[x]
 
     def join(ref):
         return [ref[x][:, :nodes] for x in range(rows)]
@@ -154,15 +159,12 @@
         for base in range(0, NR, 8):
             basis_ref[1, row, base : base + 8, :] = 0.5 * image(0, row, base)
 
-    def advance(step, carry):
+    for step in range(1, ITERS - 1):
         for row in range(8):
             for base in range(0, NR, 8):
                 basis_ref[step + 1, row, base : base + 8, :] = (
                     image(step, row, base) - basis_ref[step - 1, row, base : base + 8, :]
                 )
-        return carry
-
-    lax.fori_loop(1, ITERS - 1, advance, 0)
     for row in range(8):
         for base in range(0, NR, 8):
             last_ref[row, base : base + 8, :] = (
@@ -608,17 +610,24 @@
     hbm = pl.BlockSpec(memory_space=pltpu.HBM)
     params = pltpu.CompilerParams(vmem_limit_bytes=24 << 20)
 
-    send, up, down = pl.pallas_call(
+    send, up, down, conc_copy, diff_copy = pl.pallas_call(
         pack_kernel,
         out_shape=(
             jax.ShapeDtypeStruct((pairs * ys, LANES), f32),
             jax.ShapeDtypeStruct((EDGE, LANES), f32),
             jax.ShapeDtypeStruct((EDGE, LANES), f32),
+            jax.ShapeDtypeStruct(rhs_conc.shape, f32),
+            jax.ShapeDtypeStruct(diffusion.shape, f32),
         ),
         compiler_params=params,
     )(rhs_conc, rhs_pots, diffusion, exchange, slope)
-    left = lax.ppermute(up, "gy", [(i, i + 1) for i in range(gy - 1)])
-    right = lax.ppermute(down, "gy", [(i + 1, i) for i in range(gy - 1)])
+    even = lax.axis_index("gy") % 2 == 0
+    swaps = [
+        [pair for i in range(first, gy - 1, 2) for pair in ((i, i + 1), (i + 1, i))]
+        for first in (0, 1)
+    ]
+    one = lax.ppermute(jnp.where(even, up, down), "gy", swaps[0])
+    two = lax.ppermute(jnp.where(even, down, up), "gy", swaps[1])
     basis, coefs, deep, inner_gram = pl.pallas_call(
         free_kernel,
         out_shape=(
@@ -633,8 +642,9 @@
         ],
         compiler_params=params,
         cost_estimate=pl.CostEstimate(flops=20000000, transcendentals=0, bytes_accessed=3000000),
-    )(rhs_conc, diffusion)
-    left, right, inner_gram = lax.optimization_barrier((left, right, inner_gram))
+    )(conc_copy, diff_copy)
+    one, two, inner_gram = lax.optimization_barrier((one, two, inner_gram))
+    left, right = jnp.where(even, two, one), jnp.where(even, one, two)
     block = jnp.concatenate([send, left, right], axis=0)
     everything = lax.all_gather(block, "gx", axis=0, tiled=False)
     spot = lax.axis_index("gx").astype(jnp.int32).reshape(1)

time: 43.7 us -> 38.8 us (0.89)
  blocking collectives: 23.5 us -> 20.5 us
  Pallas kernels: 12 us -> 9.77 us
    all_to_all x1, blocking collectives: 13 us -> 9.98 us  [shards(): sums = lax.all_to_all(gram, ('gx', 'gy'), 0, 0, tiled=True)]
    pallas_call x1, Pallas kernels: 4.34 us -> 2.13 us  [shards(): pl.pallas_call(free_kernel, out_shape=(jax.ShapeDtypeStruct((ITERS, 8, NR...]
  transfers between devices with their start and end apart: 2 -> 2, of which waited for: 1 -> 0; matrix products, arithmetic and copies ran while one was open for 0% -> 0% of each run, Pallas kernels for 10% -> 6%
where the time goes in v5:
time: 38.8 us; the launch traced here: 38.6 us
  blocking collectives  20.5 us (53%)
  Pallas kernels  9.77 us (25%)
  starting transfers between devices  6.6 us (17%)
  between operations  0.86 us (2%)
  loops' own time  0.79 us (2%)
    all_gather x1, blocking collectives, shards(): everything = lax.all_gather(block, 'gx', axis=0, tiled=False)  10.5 us
    all_to_all x1, blocking collectives, shards(): sums = lax.all_to_all(gram, ('gx', 'gy'), 0, 0, tiled=True)  9.98 us
    ppermute x1, starting transfers between devices, shards(): one = lax.ppermute(jnp.where(even, up, down), 'gy', swaps[0])  5.94 us
    pallas_call x1, Pallas kernels, shards(): pl.pallas_call(functools.partial(powers_kernel, rows=rows, nodes=nodes),...  4.02 us
    pallas_call x1, Pallas kernels, shards(): pl.pallas_call(solve_kernel, out_shape=(jax.ShapeDtypeStruct(rhs_conc.sha...  2.18 us
    pallas_call x1, Pallas kernels, shards(): pl.pallas_call(free_kernel, out_shape=(jax.ShapeDtypeStruct((ITERS, 8, NR...  2.13 us
    pallas_call x1, Pallas kernels, shards(): pl.pallas_call(pack_kernel, out_shape=(jax.ShapeDtypeStruct((pairs * ys,...  1.45 us
    another operation x1, loops' own time, shards(): lax.while_loop(lambda carry: carry[0] > 0, lambda carry: (0, *plain_cycle...  0.79 us
  transfers between devices with their start and end apart: 2, of which 0 were waited for; matrix products, arithmetic and copies ran while one was open for 0% of the time, Pallas kernels for 6%

profile of v5, /device:TPU:0, one launch (start us, length us, event | category | flops | bytes accessed | tf_op | source)
XLA Modules:
  0.0 38.6 jit_solution(6041727238234284063)
XLA Ops:
  0.6 1.4 %shard_map.68 = (f32[112,128]{1,0:T(8,128)S(1)}, f32[48,128]{1,0:T(8,128)S(1)}, f32[48,128]{1,0:T(8,128)S(1)}, f32[2,16,2048]{2,1,0:T(8,128)S(1)}, f32[2,16,32]{2,1,0:T(8,128)S(1)}) custom-call(f32[2,16,2048]{2,1,0:T(8,128)} %conc_ref.1, f32[2,16,33]{2,1,0:T(8,128)} %pots_ref.1, f32[2,16,32]{2,1,0:T(8,128)} %diff_ref.1, f32[2,16,32]{2,1,0:T(8,128)} %exch_ref.1, ...), custom_call_target="tpu_custom_call" | custom-call | tf_op jit(solution)/shard_map/pallas_call | solution.py:613
  2.1 0.7 %collective-permute-start.5 = (f32[48,128]{1,0:T(8,128)S(1)}, f32[48,128]{1,0:T(8,128)S(1)}, u32[]{:S(2)}, u32[]{:S(2)}) collective-permute-start(f32[48,128]{1,0:T(8,128)S(1)} %get-tuple-element.388), channel_id=1, source_target_pairs={{1,2},{2,1},{5,6},{6,5},{9,10},{10,9},{13,14},{14,13},{17,18},{18,... | collective-permute-start | bytes 73736 | tf_op jit(solution)/shard_map/ppermute | solution.py:630
  2.8 5.9 %collective-permute-start.4 = (f32[48,128]{1,0:T(8,128)S(1)}, f32[48,128]{1,0:T(8,128)S(1)}, u32[]{:S(2)}, u32[]{:S(2)}) collective-permute-start(f32[48,128]{1,0:T(8,128)S(1)} %get-tuple-element.389), channel_id=1, source_target_pairs={{0,1},{1,0},{2,3},{3,2},{4,5},{5,4},{6,7},{7,6},{8,9},{9,8},{10,11... | collective-permute-start | bytes 73736 | tf_op jit(solution)/shard_map/ppermute | solution.py:629
  8.7 2.1 %shard_map.69 = (f32[10,8,64,128]{3,2,1,0:T(8,128)S(1)}, f32[2,8,128]{2,1,0:T(8,128)S(1)}, f32[16,128]{1,0:T(8,128)S(1)}, f32[8,128]{1,0:T(8,128)S(1)}) custom-call(f32[2,16,2048]{2,1,0:T(8,128)S(1)} %get-tuple-element.298.conc_ref, f32[2,16,32]{2,1,0:T(8,128)S(1)} %get-tuple-element.299.diff_ref), custom_call_target="tpu_custom_call" | custom-call | flops 20000000 | bytes 3000000 | tf_op jit(solution)/shard_map/pallas_call | solution.py:631
  10.8 0.0 collective-permute-done.5
  10.9 0.0 collective-permute-done.4
  10.9 10.5 %all-gather = f32[1664,128]{1,0:T(8,128)S(1)} all-gather(f32[208,128]{1,0:T(8,128)S(1)} %pad_maximum_fusion.7), channel_id=2, replica_groups=mesh['gx'=8,'gy'=4] {'gx'}, dimensions={0}, use_global_device_ids=true | all-gather | bytes 958464 | tf_op jit(solution)/shard_map/all_gather | solution.py:649
  21.5 0.0 copy-start.6
  21.5 4.0 %shard_map.70 = (f32[10,9,16,128]{3,2,1,0:T(8,128)S(1)}, f32[32,128]{1,0:T(8,128)S(1)}) custom-call(s32[1]{0:T(128)} %bitcast.3.spot_ref, f32[8,208,128]{2,1,0:T(8,128)S(1)} %bitcast.90, f32[10,8,64,128]{3,2,1,0:T(8,128)S(1)} %get-tuple-element.303.basis_ref, f32[2,8,128]{2,1,0:T(8,128)S(1)} %get-tuple-element.304.coeft_ref, ...), custom_call_target="tpu_custom_call" | custom-call | tf_op jit(solution)/shard_map/pallas_call | solution.py:653
  25.5 10.0 %all_to_all.11 = f32[32,1,128]{2,1,0:T(1,128)S(1)} all-to-all(f32[32,1,128]{2,1,0:T(1,128)S(1)} %bitcast.92), channel_id=1, replica_groups=mesh['gx'=8,'gy'=4] {'gx','gy'}, dimensions={0} | all-to-all | bytes 32768 | tf_op jit(solution)/shard_map/all_to_all | solution.py:675
  35.5 2.2 %shard_map.71 = (f32[2,16,2048]{2,1,0:T(8,128)}, f32[2,16,33]{2,1,0:T(8,128)}, s32[1]{0:T(128)}) custom-call(f32[32,128]{1,0:T(8,128)S(1)} %bitcast.91, f32[10,8,64,128]{3,2,1,0:T(8,128)S(1)} %get-tuple-element.303.basis_ref, f32[10,9,16,128]{3,2,1,0:T(8,128)S(1)} %get-tuple-element.308.outer_ref), custom_call_target="tpu_custom_call" | custom-call | tf_op jit(solution)/shard_map/pallas_call | solution.py:677
  37.7 0.0 copy-done.6
  37.7 0.8 %while.32 = (s32[]{:T(128)}, f32[2,16,2048]{2,1,0:T(8,128)}, f32[2,16,33]{2,1,0:T(8,128)}, f32[2,16,2048]{2,1,0:T(8,128)S(1)}, f32[2,16,33]{2,1,0:T(8,128)}, /*i...) while((s32[]{:T(128)}, f32[2,16,2048]{2,1,0:T(8,128)}, ...), condition=%region_17.18_spmd, body=%region_0.17_spmd | while | flops 5869439 | bytes 33019008 | solution.py:692
  (3 shorter events, 0.1 us)
Async XLA Ops:
  2.1 8.7 %collective-permute-start.5 = (f32[48,128]{1,0:T(8,128)S(1)}, f32[48,128]{1,0:T(8,128)S(1)}, u32[]{:S(2)}, u32[]{:S(2)}) collective-permute-start(f32[48,128]{1,0:T(8,128)S(1)} %get-tuple-element.388), channel_id=1, source_target_pairs={{1,2},{2,1},{5,6},{6,5},{9,10},{10,9},{13,14},{14,13},{17,18},{18,... | collective-permute-start | bytes 73736 | tf_op jit(solution)/shard_map/ppermute | solution.py:630
  2.8 8.1 %collective-permute-start.4 = (f32[48,128]{1,0:T(8,128)S(1)}, f32[48,128]{1,0:T(8,128)S(1)}, u32[]{:S(2)}, u32[]{:S(2)}) collective-permute-start(f32[48,128]{1,0:T(8,128)S(1)} %get-tuple-element.389), channel_id=1, source_target_pairs={{0,1},{1,0},{2,3},{3,2},{4,5},{5,4},{6,7},{7,6},{8,9},{9,8},{10,11... | collective-permute-start | bytes 73736 | tf_op jit(solution)/shard_map/ppermute | solution.py:629
  21.5 16.2 %copy-start.6 = (f32[2,16,2048]{2,1,0:T(8,128)S(1)}, f32[2,16,2048]{2,1,0:T(8,128)}, u32[]{:S(2)}) copy-start(f32[2,16,2048]{2,1,0:T(8,128)} %conc_ref.1) | copy-start | bytes 786436

commit v6 on v5

--- a/solution.py
+++ b/solution.py
@@ -333,20 +333,22 @@
         GAIN * turn_nodes(turned[step * ys // LANES], step * ys % LANES, rows, ys, nodes)
         for step in range(ITERS)
     ]
-    sub = lax.broadcasted_iota(jnp.int32, (24, LANES), 0)
+    tall = (16, LANES)
+    sub = lax.broadcasted_iota(jnp.int32, tall, 0)
     for row in range(8):
-        gain = jnp.broadcast_to(coeft_ref[0, row : row + 1, :], (24, LANES))
-        keep = jnp.broadcast_to(coeft_ref[1, row : row + 1, :], (24, LANES))
-        now, old = basis_ref[0, row, NR - 24 :, :], None
-        outer_ref[0, row] = now[8:]
+        gain = jnp.broadcast_to(coeft_ref[0, row : row + 1, :], tall)
+        keep = jnp.broadcast_to(coeft_ref[1, row : row + 1, :], tall)
+        now, old = basis_ref[0, row, NR - 16 :, :], None
+        outer_ref[0, row] = now
         for step in range(ITERS):
-            prev = jnp.where(sub == 0, now, pltpu.roll(now, 1, 0))
-            following = jnp.where(sub == 23, now, pltpu.roll(now, 23, 0))
-            flow = jnp.broadcast_to(flows[step][row : row + 1, :], (24, LANES))
-            value = keep * now - gain * (prev + following) + jnp.where(sub == 23, flow, 0.0)
+            above = jnp.broadcast_to(basis_ref[step, row, NR - 17 : NR - 16, :], tall)
+            prev = jnp.where(sub == 0, above, pltpu.roll(now, 1, 0))
+            following = jnp.where(sub == 15, now, pltpu.roll(now, 15, 0))
+            flow = jnp.broadcast_to(flows[step][row : row + 1, :], tall)
+            value = keep * now - gain * (prev + following) + jnp.where(sub == 15, flow, 0.0)
             value = 0.5 * value if step == 0 else value - old
             now, old = value, now
-            room_for(step + 1)[row] = now[8:]
+            room_for(step + 1)[row] = now
 
     acc_ref[...] = jnp.zeros(acc_ref.shape, jnp.float32)
     inside = jnp.where(lax.broadcasted_iota(jnp.int32, (16, LANES), 0) >= 16 - ITERS, 1.0, 0.0)

time: 38.8 us -> 38.7 us (level)
  no operation moved by 1% of the time
where the time goes in v6:
time: 38.7 us; the launch traced here: 38.5 us
  blocking collectives  20.5 us (53%)
  Pallas kernels  9.69 us (25%)
  starting transfers between devices  6.6 us (17%)
  between operations  0.86 us (2%)
  loops' own time  0.79 us (2%)
    all_gather x1, blocking collectives, shards(): everything = lax.all_gather(block, 'gx', axis=0, tiled=False)  10.5 us
    all_to_all x1, blocking collectives, shards(): sums = lax.all_to_all(gram, ('gx', 'gy'), 0, 0, tiled=True)  9.98 us
    ppermute x1, starting transfers between devices, shards(): one = lax.ppermute(jnp.where(even, up, down), 'gy', swaps[0])  5.94 us
    pallas_call x1, Pallas kernels, shards(): pl.pallas_call(functools.partial(powers_kernel, rows=rows, nodes=nodes),...  3.94 us
    pallas_call x1, Pallas kernels, shards(): pl.pallas_call(solve_kernel, out_shape=(jax.ShapeDtypeStruct(rhs_conc.sha...  2.18 us
    pallas_call x1, Pallas kernels, shards(): pl.pallas_call(free_kernel, out_shape=(jax.ShapeDtypeStruct((ITERS, 8, NR...  2.13 us
    pallas_call x1, Pallas kernels, shards(): pl.pallas_call(pack_kernel, out_shape=(jax.ShapeDtypeStruct((pairs * ys,...  1.45 us
    another operation x1, loops' own time, shards(): lax.while_loop(lambda carry: carry[0] > 0, lambda carry: (0, *plain_cycle...  0.79 us
  transfers between devices with their start and end apart: 2, of which 0 were waited for; matrix products, arithmetic and copies ran while one was open for 0% of the time, Pallas kernels for 6%

profile of v6, /device:TPU:0, one launch (start us, length us, event | category | flops | bytes accessed | tf_op | source)
XLA Modules:
  0.0 38.5 jit_solution(2956537439484698046)
XLA Ops:
  0.6 1.4 %shard_map.68 = (f32[112,128]{1,0:T(8,128)S(1)}, f32[48,128]{1,0:T(8,128)S(1)}, f32[48,128]{1,0:T(8,128)S(1)}, f32[2,16,2048]{2,1,0:T(8,128)S(1)}, f32[2,16,32]{2,1,0:T(8,128)S(1)}) custom-call(f32[2,16,2048]{2,1,0:T(8,128)} %conc_ref.1, f32[2,16,33]{2,1,0:T(8,128)} %pots_ref.1, f32[2,16,32]{2,1,0:T(8,128)} %diff_ref.1, f32[2,16,32]{2,1,0:T(8,128)} %exch_ref.1, ...), custom_call_target="tpu_custom_call" | custom-call | tf_op jit(solution)/shard_map/pallas_call | solution.py:615
  2.1 0.7 %collective-permute-start.5 = (f32[48,128]{1,0:T(8,128)S(1)}, f32[48,128]{1,0:T(8,128)S(1)}, u32[]{:S(2)}, u32[]{:S(2)}) collective-permute-start(f32[48,128]{1,0:T(8,128)S(1)} %get-tuple-element.388), channel_id=1, source_target_pairs={{1,2},{2,1},{5,6},{6,5},{9,10},{10,9},{13,14},{14,13},{17,18},{18,... | collective-permute-start | bytes 73736 | tf_op jit(solution)/shard_map/ppermute | solution.py:632
  2.8 5.9 %collective-permute-start.4 = (f32[48,128]{1,0:T(8,128)S(1)}, f32[48,128]{1,0:T(8,128)S(1)}, u32[]{:S(2)}, u32[]{:S(2)}) collective-permute-start(f32[48,128]{1,0:T(8,128)S(1)} %get-tuple-element.389), channel_id=1, source_target_pairs={{0,1},{1,0},{2,3},{3,2},{4,5},{5,4},{6,7},{7,6},{8,9},{9,8},{10,11... | collective-permute-start | bytes 73736 | tf_op jit(solution)/shard_map/ppermute | solution.py:631
  8.7 2.1 %shard_map.69 = (f32[10,8,64,128]{3,2,1,0:T(8,128)S(1)}, f32[2,8,128]{2,1,0:T(8,128)S(1)}, f32[16,128]{1,0:T(8,128)S(1)}, f32[8,128]{1,0:T(8,128)S(1)}) custom-call(f32[2,16,2048]{2,1,0:T(8,128)S(1)} %get-tuple-element.298.conc_ref, f32[2,16,32]{2,1,0:T(8,128)S(1)} %get-tuple-element.299.diff_ref), custom_call_target="tpu_custom_call" | custom-call | flops 20000000 | bytes 3000000 | tf_op jit(solution)/shard_map/pallas_call | solution.py:633
  10.8 0.0 collective-permute-done.5
  10.9 0.0 collective-permute-done.4
  10.9 10.5 %all-gather = f32[1664,128]{1,0:T(8,128)S(1)} all-gather(f32[208,128]{1,0:T(8,128)S(1)} %pad_maximum_fusion.7), channel_id=2, replica_groups=mesh['gx'=8,'gy'=4] {'gx'}, dimensions={0}, use_global_device_ids=true | all-gather | bytes 958464 | tf_op jit(solution)/shard_map/all_gather | solution.py:651
  21.5 0.0 copy-start.6
  21.5 3.9 %shard_map.70 = (f32[10,9,16,128]{3,2,1,0:T(8,128)S(1)}, f32[32,128]{1,0:T(8,128)S(1)}) custom-call(s32[1]{0:T(128)} %bitcast.3.spot_ref, f32[8,208,128]{2,1,0:T(8,128)S(1)} %bitcast.90, f32[10,8,64,128]{3,2,1,0:T(8,128)S(1)} %get-tuple-element.303.basis_ref, f32[2,8,128]{2,1,0:T(8,128)S(1)} %get-tuple-element.304.coeft_ref, ...), custom_call_target="tpu_custom_call" | custom-call | tf_op jit(solution)/shard_map/pallas_call | solution.py:655
  25.4 10.0 %all_to_all.11 = f32[32,1,128]{2,1,0:T(1,128)S(1)} all-to-all(f32[32,1,128]{2,1,0:T(1,128)S(1)} %bitcast.92), channel_id=1, replica_groups=mesh['gx'=8,'gy'=4] {'gx','gy'}, dimensions={0} | all-to-all | bytes 32768 | tf_op jit(solution)/shard_map/all_to_all | solution.py:677
  35.4 2.2 %shard_map.71 = (f32[2,16,2048]{2,1,0:T(8,128)}, f32[2,16,33]{2,1,0:T(8,128)}, s32[1]{0:T(128)}) custom-call(f32[32,128]{1,0:T(8,128)S(1)} %bitcast.91, f32[10,8,64,128]{3,2,1,0:T(8,128)S(1)} %get-tuple-element.303.basis_ref, f32[10,9,16,128]{3,2,1,0:T(8,128)S(1)} %get-tuple-element.308.outer_ref), custom_call_target="tpu_custom_call" | custom-call | tf_op jit(solution)/shard_map/pallas_call | solution.py:679
  37.6 0.0 copy-done.6
  37.6 0.8 %while.32 = (s32[]{:T(128)}, f32[2,16,2048]{2,1,0:T(8,128)}, f32[2,16,33]{2,1,0:T(8,128)}, f32[2,16,2048]{2,1,0:T(8,128)S(1)}, f32[2,16,33]{2,1,0:T(8,128)}, /*i...) while((s32[]{:T(128)}, f32[2,16,2048]{2,1,0:T(8,128)}, ...), condition=%region_17.18_spmd, body=%region_0.17_spmd | while | flops 5869439 | bytes 33019008 | solution.py:694
  (3 shorter events, 0.1 us)
Async XLA Ops:
  2.1 8.7 %collective-permute-start.5 = (f32[48,128]{1,0:T(8,128)S(1)}, f32[48,128]{1,0:T(8,128)S(1)}, u32[]{:S(2)}, u32[]{:S(2)}) collective-permute-start(f32[48,128]{1,0:T(8,128)S(1)} %get-tuple-element.388), channel_id=1, source_target_pairs={{1,2},{2,1},{5,6},{6,5},{9,10},{10,9},{13,14},{14,13},{17,18},{18,... | collective-permute-start | bytes 73736 | tf_op jit(solution)/shard_map/ppermute | solution.py:632
  2.8 8.1 %collective-permute-start.4 = (f32[48,128]{1,0:T(8,128)S(1)}, f32[48,128]{1,0:T(8,128)S(1)}, u32[]{:S(2)}, u32[]{:S(2)}) collective-permute-start(f32[48,128]{1,0:T(8,128)S(1)} %get-tuple-element.389), channel_id=1, source_target_pairs={{0,1},{1,0},{2,3},{3,2},{4,5},{5,4},{6,7},{7,6},{8,9},{9,8},{10,11... | collective-permute-start | bytes 73736 | tf_op jit(solution)/shard_map/ppermute | solution.py:631
  21.5 16.1 %copy-start.6 = (f32[2,16,2048]{2,1,0:T(8,128)S(1)}, f32[2,16,2048]{2,1,0:T(8,128)}, u32[]{:S(2)}) copy-start(f32[2,16,2048]{2,1,0:T(8,128)} %conc_ref.1) | copy-start | bytes 786436

commit v7 on v6

--- a/solution.py
+++ b/solution.py
@@ -674,7 +674,7 @@
         compiler_params=params,
     )(spot, everything, basis, coefs, deep, inner_gram)
 
-    sums = lax.all_to_all(gram, ("gx", "gy"), 0, 0, tiled=True)
+    sums = lax.all_to_all(gram, ("gy", "gx"), 0, 0, tiled=True)
 
     conc, pots, flag = pl.pallas_call(
         solve_kernel,

time: 38.7 us -> 38.7 us (level)
  no operation moved by 1% of the time
where the time goes in v7:
time: 38.7 us; the launch traced here: 38.5 us
  blocking collectives  20.5 us (53%)
  Pallas kernels  9.69 us (25%)
  starting transfers between devices  6.6 us (17%)
  between operations  0.86 us (2%)
  loops' own time  0.79 us (2%)
    all_gather x1, blocking collectives, shards(): everything = lax.all_gather(block, 'gx', axis=0, tiled=False)  10.5 us
    all_to_all x1, blocking collectives, shards(): sums = lax.all_to_all(gram, ('gy', 'gx'), 0, 0, tiled=True)  9.96 us
    ppermute x1, starting transfers between devices, shards(): one = lax.ppermute(jnp.where(even, up, down), 'gy', swaps[0])  5.94 us
    pallas_call x1, Pallas kernels, shards(): pl.pallas_call(functools.partial(powers_kernel, rows=rows, nodes=nodes),...  3.94 us
    pallas_call x1, Pallas kernels, shards(): pl.pallas_call(solve_kernel, out_shape=(jax.ShapeDtypeStruct(rhs_conc.sha...  2.18 us
    pallas_call x1, Pallas kernels, shards(): pl.pallas_call(free_kernel, out_shape=(jax.ShapeDtypeStruct((ITERS, 8, NR...  2.13 us
    pallas_call x1, Pallas kernels, shards(): pl.pallas_call(pack_kernel, out_shape=(jax.ShapeDtypeStruct((pairs * ys,...  1.45 us
    another operation x1, loops' own time, shards(): lax.while_loop(lambda carry: carry[0] > 0, lambda carry: (0, *plain_cycle...  0.79 us
  transfers between devices with their start and end apart: 2, of which 0 were waited for; matrix products, arithmetic and copies ran while one was open for 0% of the time, Pallas kernels for 6%

profile of v7, /device:TPU:0, one launch (start us, length us, event | category | flops | bytes accessed | tf_op | source)
XLA Modules:
  0.0 38.5 jit_solution(1476222535629485148)
XLA Ops:
  0.6 1.4 %shard_map.68 = (f32[112,128]{1,0:T(8,128)S(1)}, f32[48,128]{1,0:T(8,128)S(1)}, f32[48,128]{1,0:T(8,128)S(1)}, f32[2,16,2048]{2,1,0:T(8,128)S(1)}, f32[2,16,32]{2,1,0:T(8,128)S(1)}) custom-call(f32[2,16,2048]{2,1,0:T(8,128)} %conc_ref.1, f32[2,16,33]{2,1,0:T(8,128)} %pots_ref.1, f32[2,16,32]{2,1,0:T(8,128)} %diff_ref.1, f32[2,16,32]{2,1,0:T(8,128)} %exch_ref.1, ...), custom_call_target="tpu_custom_call" | custom-call | tf_op jit(solution)/shard_map/pallas_call | solution.py:615
  2.1 0.7 %collective-permute-start.5 = (f32[48,128]{1,0:T(8,128)S(1)}, f32[48,128]{1,0:T(8,128)S(1)}, u32[]{:S(2)}, u32[]{:S(2)}) collective-permute-start(f32[48,128]{1,0:T(8,128)S(1)} %get-tuple-element.388), channel_id=1, source_target_pairs={{1,2},{2,1},{5,6},{6,5},{9,10},{10,9},{13,14},{14,13},{17,18},{18,... | collective-permute-start | bytes 73736 | tf_op jit(solution)/shard_map/ppermute | solution.py:632
  2.8 5.9 %collective-permute-start.4 = (f32[48,128]{1,0:T(8,128)S(1)}, f32[48,128]{1,0:T(8,128)S(1)}, u32[]{:S(2)}, u32[]{:S(2)}) collective-permute-start(f32[48,128]{1,0:T(8,128)S(1)} %get-tuple-element.389), channel_id=1, source_target_pairs={{0,1},{1,0},{2,3},{3,2},{4,5},{5,4},{6,7},{7,6},{8,9},{9,8},{10,11... | collective-permute-start | bytes 73736 | tf_op jit(solution)/shard_map/ppermute | solution.py:631
  8.7 2.1 %shard_map.69 = (f32[10,8,64,128]{3,2,1,0:T(8,128)S(1)}, f32[2,8,128]{2,1,0:T(8,128)S(1)}, f32[16,128]{1,0:T(8,128)S(1)}, f32[8,128]{1,0:T(8,128)S(1)}) custom-call(f32[2,16,2048]{2,1,0:T(8,128)S(1)} %get-tuple-element.298.conc_ref, f32[2,16,32]{2,1,0:T(8,128)S(1)} %get-tuple-element.299.diff_ref), custom_call_target="tpu_custom_call" | custom-call | flops 20000000 | bytes 3000000 | tf_op jit(solution)/shard_map/pallas_call | solution.py:633
  10.8 0.0 collective-permute-done.5
  10.9 0.0 collective-permute-done.4
  10.9 10.5 %all-gather = f32[1664,128]{1,0:T(8,128)S(1)} all-gather(f32[208,128]{1,0:T(8,128)S(1)} %pad_maximum_fusion.7), channel_id=2, replica_groups=mesh['gx'=8,'gy'=4] {'gx'}, dimensions={0}, use_global_device_ids=true | all-gather | bytes 958464 | tf_op jit(solution)/shard_map/all_gather | solution.py:651
  21.5 0.0 copy-start.6
  21.5 3.9 %shard_map.70 = (f32[10,9,16,128]{3,2,1,0:T(8,128)S(1)}, f32[32,128]{1,0:T(8,128)S(1)}) custom-call(s32[1]{0:T(128)} %bitcast.3.spot_ref, f32[8,208,128]{2,1,0:T(8,128)S(1)} %bitcast.90, f32[10,8,64,128]{3,2,1,0:T(8,128)S(1)} %get-tuple-element.303.basis_ref, f32[2,8,128]{2,1,0:T(8,128)S(1)} %get-tuple-element.304.coeft_ref, ...), custom_call_target="tpu_custom_call" | custom-call | tf_op jit(solution)/shard_map/pallas_call | solution.py:655
  25.4 10.0 %all_to_all.11 = f32[32,1,128]{2,1,0:T(1,128)S(1)} all-to-all(f32[32,1,128]{2,1,0:T(1,128)S(1)} %bitcast.92), channel_id=1, replica_groups=mesh['gx'=8,'gy'=4] {'gy','gx'}, dimensions={0} | all-to-all | bytes 32768 | tf_op jit(solution)/shard_map/all_to_all | solution.py:677
  35.4 2.2 %shard_map.71 = (f32[2,16,2048]{2,1,0:T(8,128)}, f32[2,16,33]{2,1,0:T(8,128)}, s32[1]{0:T(128)}) custom-call(f32[32,128]{1,0:T(8,128)S(1)} %bitcast.91, f32[10,8,64,128]{3,2,1,0:T(8,128)S(1)} %get-tuple-element.303.basis_ref, f32[10,9,16,128]{3,2,1,0:T(8,128)S(1)} %get-tuple-element.308.outer_ref), custom_call_target="tpu_custom_call" | custom-call | tf_op jit(solution)/shard_map/pallas_call | solution.py:679
  37.6 0.0 copy-done.6
  37.6 0.8 %while.32 = (s32[]{:T(128)}, f32[2,16,2048]{2,1,0:T(8,128)}, f32[2,16,33]{2,1,0:T(8,128)}, f32[2,16,2048]{2,1,0:T(8,128)S(1)}, f32[2,16,33]{2,1,0:T(8,128)}, /*i...) while((s32[]{:T(128)}, f32[2,16,2048]{2,1,0:T(8,128)}, ...), condition=%region_17.18_spmd, body=%region_0.17_spmd | while | flops 5869439 | bytes 33019008 | solution.py:694
  (3 shorter events, 0.1 us)
Async XLA Ops:
  2.1 8.7 %collective-permute-start.5 = (f32[48,128]{1,0:T(8,128)S(1)}, f32[48,128]{1,0:T(8,128)S(1)}, u32[]{:S(2)}, u32[]{:S(2)}) collective-permute-start(f32[48,128]{1,0:T(8,128)S(1)} %get-tuple-element.388), channel_id=1, source_target_pairs={{1,2},{2,1},{5,6},{6,5},{9,10},{10,9},{13,14},{14,13},{17,18},{18,... | collective-permute-start | bytes 73736 | tf_op jit(solution)/shard_map/ppermute | solution.py:632
  2.8 8.1 %collective-permute-start.4 = (f32[48,128]{1,0:T(8,128)S(1)}, f32[48,128]{1,0:T(8,128)S(1)}, u32[]{:S(2)}, u32[]{:S(2)}) collective-permute-start(f32[48,128]{1,0:T(8,128)S(1)} %get-tuple-element.389), channel_id=1, source_target_pairs={{0,1},{1,0},{2,3},{3,2},{4,5},{5,4},{6,7},{7,6},{8,9},{9,8},{10,11... | collective-permute-start | bytes 73736 | tf_op jit(solution)/shard_map/ppermute | solution.py:631
  21.5 16.1 %copy-start.6 = (f32[2,16,2048]{2,1,0:T(8,128)S(1)}, f32[2,16,2048]{2,1,0:T(8,128)}, u32[]{:S(2)}) copy-start(f32[2,16,2048]{2,1,0:T(8,128)} %conc_ref.1) | copy-start | bytes 786436
